TPU v7x, 128 devices: a whole 4x4x4 slice. The times are simulated.
128 devices in a mesh: gx: 4 (over x_hi, core), gy: 4 (over y), gz: 8 (over z, x_lo).
Axes of the slice: x: 4 (x_hi: 2, x_lo: 2; x = x_hi * 2 + x_lo), y: 4, z: 4, core: 2. Of those that a mesh axis runs over, the one named last changes fastest.
Arguments:
- field: float32 [64, 1024, 1024], P('gx', 'gy', 'gz'), may hold values from -6 to 6
- source: float32 [64, 1024, 1024], P('gx', 'gy', 'gz'), may hold values from -6 to 6
Outputs:
- smoothed: float32 [64, 1024, 1024], P('gx', 'gy', 'gz')
All inputs are finite; a program needn't handle non-finite values.
Results may differ from a plain program's by a relative error of at most 0.00002.
Values sent between devices are 32-bit elements; how exact they have to be, the bound alone decides.
No kernel may reach another device: no remote copies, remote signals or barrier semaphores. Data moves between devices by JAX's collectives and lax.ppermute only.
A program may use at most 64 MiB of HBM per device.

v0:
```python
import jax
import jax.numpy as jnp
from jax import lax
from jax.experimental import pallas as pl
from jax.experimental.pallas import tpu as pltpu
from jax.sharding import PartitionSpec as P

F32 = jnp.float32
VM = pltpu.VMEM
Q, NY, NZ = 8, 256, 128
ROWS = NY + 32
TILES = NY // 8
SIXTH = 1.0 / 6.0
SUB = 8


def lanes_of():
    return lax.broadcasted_iota(jnp.int32, (8, 128), 1)


def odd_cells():
    return (lax.broadcasted_iota(jnp.int32, (8, 128), 0) + lanes_of()) % 2


def turn(value, shift):
    shift = shift % 128
    return value if shift == 0 else pltpu.roll(value, shift, 1)


def mirrored(q, flip):
    return q + flip * (Q - 1 - 2 * q)


CHUNKS = 4


def pack_kernel(flip_ref, field, source, bm, srm, sbm, high, low, zlow, zhigh, fbuf, sbuf, sems):
    flip = flip_ref[0]
    span = NY // CHUNKS
    copies = []
    for c in range(CHUNKS):
        rows = pl.ds(c * span, span)
        for n, (src, dst) in enumerate(((field, fbuf), (source, sbuf))):
            copy = pltpu.make_async_copy(src.at[:, :, rows, :], dst.at[:, :, rows, :], sems.at[2 * c + n])
            copy.start()
            copies.append(copy)
    odd = odd_cells() == 1
    lane = lanes_of()
    col = lane % 16
    left_half = lane < 64

    def tile(t, carry):
        r = pl.multiple_of(t * 8, 8)
        rows = pl.ds(r, 8)
        put = pl.ds(pl.multiple_of(r + 16, 8), 8)
        acc = [jnp.zeros((8, 128), F32)] * 4
        for q in range(Q):
            at = mirrored(q, flip)
            f0, f1 = fbuf[at, 0, rows, :], fbuf[at, 1, rows, :]
            s0, s1 = sbuf[at, 0, rows, :], sbuf[at, 1, rows, :]
            b = jnp.where(odd, f0, f1)
            sr = jnp.where(odd, s1, s0)
            sb = jnp.where(odd, s0, s1)
            bm[q, put, :] = b
            srm[q, put, :] = sr
            sbm[q, put, :] = sb
            for out, d in ((low, q), (high, Q - 1 - q)):
                if d < 3:
                    out[d, rows, :] = b
                    out[3 + d, rows, :] = sr
                if d < 2:
                    out[6 + d, rows, :] = sb
            here = lane // 16 == q
            parts = (
                turn(b, 16 * q),
                turn(jnp.where(left_half, sr, b), 16 * q + 6),
                turn(jnp.where(left_half, sb, sr), 16 * q + 11),
                turn(sb, 16 * q + 15),
            )
            acc = [jnp.where(here, new, old) for new, old in zip(parts, acc)]
        zlow[rows, :] = jnp.where(col < 6, acc[0], jnp.where(col < 11, acc[1], acc[2]))
        zhigh[rows, :] = jnp.where(col < 6, acc[1], jnp.where(col < 11, acc[2], acc[3]))
        return carry

    for c in range(CHUNKS):
        copies[2 * c].wait()
        copies[2 * c + 1].wait()
        lax.fori_loop(c * span // 8, (c + 1) * span // 8, tile, 0)


def y_kernel(bm, srm, sbm, zr, zl, ylow, yhigh):
    for out, row in ((ylow, 0), (yhigh, NY - 8)):
        for n, ref in enumerate((bm, srm, sbm)):
            for q in range(Q):
                out[8 * n + q] = ref[q, row + 16:row + 24, :]
        out[24] = zr[row:row + 8, :]
        out[25] = zl[row:row + 8, :]


def corner_kernel(yr, yl, zr, zl, high, low):
    lane = lanes_of()
    left_half = lane < 64
    for out, planes in ((low, (0, 1, 2)), (high, (7, 6, 5))):
        for side, ref in enumerate((yr, yl)):
            for d, q in enumerate(planes):
                out[8 * side + d] = ref[q]
                out[8 * side + 3 + d] = ref[8 + q]
                if d < 2:
                    out[8 * side + 6 + d] = ref[16 + q]

    def put(n, r, l):
        low[n] = jnp.where(left_half, r, turn(l, 64))
        high[n] = jnp.where(left_half, turn(r, 48), turn(l, 112))

    def tile(t, carry):
        rows = pl.ds(pl.multiple_of(t * 8, 8), 8)
        put(t + 17, zr[rows, :], zl[rows, :])
        return carry

    put(16, yl[24], yl[25])
    put(49, yr[24], yr[25])
    lax.fori_loop(0, TILES, tile, 0)


def mirror_jobs(jobs):
    swap = {"both": "both", "up": "down", "down": "up"}
    return [(Q - 1 - q, swap[x], None if keep is None else 1 - keep) for q, x, keep in jobs]


def half_sweep(r, red, jobs, odd, lane, get, factor, rims=True):
    first, last = lane == 0, lane == 127
    rows = pl.ds(r, 8)
    above, below = pl.ds(r - 1, 8), pl.ds(r + 1, 8)
    centre = {}

    def at(q):
        if q not in centre:
            main, rim = get("black" if red else "red", q)
            centre[q] = (main[rows, :], rim[rows, :] if rims else None)
        return centre[q]

    done = {}
    for q, x, keep in jobs:
        mains = get("black" if red else "red", q)
        sources = get("sr" if red else "sb", q)
        olds = get("red" if red else "black", q)
        cm = at(q)[0]
        ch = at(q)[1] if rims else mains[1][rows, :]
        lm, lh = turn(cm, 1), turn(ch, 1)
        rm, rh = turn(cm, 127), turn(ch, 127)
        beside = (
            jnp.where(first, lh, lm) + jnp.where(last, rh, rm),
            jnp.where(first, lm, lh) + jnp.where(last, rm, rh) if rims else None,
        )
        new = []
        for n in range(2 if rims else 1):
            if x == "up":
                along = at(q + 1)[n]
            elif x == "down":
                along = at(q - 1)[n]
            elif red:
                along = jnp.where(odd, at(q + 1)[n], at(q - 1)[n])
            else:
                along = jnp.where(odd, at(q - 1)[n], at(q + 1)[n])
            total = (sources[n][rows, :] + at(q)[n]) + (along + beside[n])
            total = total + (mains[n][above, :] + mains[n][below, :])
            value = total * factor(q)
            if keep == 1:
                value = jnp.where(odd, olds[n][rows, :], value)
            elif keep == 0:
                value = jnp.where(odd, value, olds[n][rows, :])
            new.append(value)
        done[q] = new
    return done


def sweep_rows(red, jobs, odd, lane, get, factor):
    def tile(t, carry):
        r = pl.multiple_of(t * 8 + 8, 8)
        for q, new in half_sweep(r, red, jobs, odd, lane, get, factor).items():
            for ref, value in zip(get("red" if red else "black", q), new):
                ref[pl.ds(r, 8), :] = value
        return carry

    lax.fori_loop(0, TILES + 2, tile, 0)


def full(*qs):
    return [(q, "both", None) for q in qs]


def inner_kernel(flip_ref, bm_in, srm_in, sbm_in, yr, yl, zr, zl, bm, rm, srm, sbm, bh, rh, srh, sbh):
    del bm_in, srm_in, sbm_in
    lane = lanes_of()
    odd = (odd_cells() + flip_ref[0]) % 2 == 1
    col = lane % 16

    for row, ref in ((8, yl), (NY + 16, yr)):
        for q in range(Q):
            bm[q, row:row + 8, :] = ref[q]
            srm[q, row:row + 8, :] = ref[8 + q]
            sbm[q, row:row + 8, :] = ref[16 + q]

    def rim(rows, r, l):
        one = jnp.where(col < 6, l, r)
        two = jnp.where(col < 11, l, r)
        for q in range(Q):
            parts = [turn(r, -16 * q), turn(one, -16 * q - 6), turn(two, -16 * q - 11), turn(l, 113 - 16 * q)]
            for n, (ref, width) in enumerate(((bh, 6), (srh, 5), (sbh, 4))):
                ref[q, rows, :] = jnp.where(lane < width, parts[n], jnp.where(lane >= 128 - width, parts[n + 1], 0.0))

    rim(pl.ds(8, 8), yl[24], yl[25])
    rim(pl.ds(NY + 16, 8), yr[24], yr[25])

    def tile(t, carry):
        r = pl.multiple_of(t * 8, 8)
        rim(pl.ds(pl.multiple_of(r + 16, 8), 8), zr[pl.ds(r, 8), :], zl[pl.ds(r, 8), :])
        return carry

    lax.fori_loop(0, TILES, tile, 0)

    table = {"black": (bm, bh), "red": (rm, rh), "sr": (srm, srh), "sb": (sbm, sbh)}

    def get(kind, q):
        return [ref.at[q] for ref in table[kind]]

    def factor(q):
        return SIXTH

    edge1, edge3, edge5 = [(0, "up", None)], [(1, "up", 0)], [(2, "up", 0)]
    for red, jobs in (
        (True, edge1 + full(*range(1, 7)) + mirror_jobs(edge1)),
        (False, full(*range(1, 7))),
        (True, edge3 + full(*range(2, 6)) + mirror_jobs(edge3)),
        (False, full(*range(2, 6))),
        (True, edge5 + full(3, 4) + mirror_jobs(edge5)),
        (False, full(3, 4)),
    ):
        sweep_rows(red, jobs, odd, lane, get, factor)


OUT_CHUNKS = 4


def outer_kernel(flip_ref, wall_ref, bm_in, rm_in, srm, sbm, bh_in, rh_in, srh, sbh, high, low, chigh, clow,
                 out, bm, rm, bh, rh, xbm, xbh, xrm, xrh, xsrm, xsrh, xsbm, xsbh, obuf, sems):
    del bm_in, rm_in, bh_in, rh_in
    flip = flip_ref[0]
    wall = wall_ref[0]
    lane = lanes_of()
    plain = odd_cells() == 1
    odd = (odd_cells() + flip) % 2 == 1

    for side, main, corner in ((0, low, clow), (1, high, chigh)):
        for d in range(3):
            slot = 3 * side + d
            for n, (ref, deep) in enumerate(((xbm, 3), (xsrm, 3), (xsbm, 2))):
                if d < deep:
                    slot_n = deep * side + d
                    ref[slot_n, 8:16, :] = corner[8 + 3 * n + d]
                    ref[slot_n, 16:NY + 16, :] = main[3 * n + d]
                    ref[slot_n, NY + 16:NY + 24, :] = corner[3 * n + d]

    def rim(t, carry):
        rows = pl.ds(pl.multiple_of(t * 8 + 8, 8), 8)
        for side, corner in ((0, clow), (1, chigh)):
            both = corner[16 + t]
            for d in range(3):
                c = 16 * (d if side == 0 else 2 - d)
                for n, (ref, deep, width) in enumerate(((xbh, 3, 6), (xsrh, 3, 5), (xsbh, 2, 4))):
                    if d < deep:
                        off = c + (0, 6, 11)[n]
                        right = turn(both, -off)
                        left = turn(both, 128 - width - 64 - off)
                        ref[deep * side + d, rows, :] = jnp.where(
                            lane < width, right, jnp.where(lane >= 128 - width, left, 0.0)
                        )
        return carry

    lax.fori_loop(0, TILES + 2, rim, 0)

    own = {"black": (bm, bh), "red": (rm, rh), "sr": (srm, srh), "sb": (sbm, sbh)}
    halo = {"black": (xbm, xbh), "red": (xrm, xrh), "sr": (xsrm, xsrh), "sb": (xsbm, xsbh)}

    def get(kind, q):
        if 0 <= q < Q:
            return [ref.at[q] for ref in own[kind]]
        deep = 2 if kind == "sb" else 3
        slot = -1 - q if q < 0 else deep + q - Q
        return [ref.at[slot] for ref in halo[kind]]

    def factor(q):
        return wall if q < 0 else SIXTH

    for red, jobs in (
        (True, [(-3, "up", None)] + full(-2, -1) + [(0, "down", 1)]),
        (False, full(-2, -1, 0)),
        (True, [(-2, "up", None)] + full(-1, 0) + [(1, "down", 1)]),
        (False, full(-1, 0, 1)),
        (True, [(-1, "up", None)] + full(0, 1) + [(2, "down", 1)]),
    ):
        sweep_rows(red, jobs + mirror_jobs(jobs), odd, lane, get, factor)

    jobs = full(0, 1, 2)
    jobs = jobs + mirror_jobs(jobs)

    def tile(t, carry):
        r = pl.multiple_of(t * 8 + 16, 8)
        rows = pl.ds(pl.multiple_of(t * 8, 8), 8)
        new = half_sweep(r, False, jobs, odd, lane, get, factor, rims=False)
        for q in range(Q):
            b = new[q][0] if q in new else bm[q, pl.ds(r, 8), :]
            v = rm[q, pl.ds(r, 8), :]
            at = mirrored(q, flip)
            obuf[at, 0, rows, :] = jnp.where(plain, b, v)
            obuf[at, 1, rows, :] = jnp.where(plain, v, b)
        return carry

    span = NY // OUT_CHUNKS
    copies = []
    for c in range(OUT_CHUNKS):
        lax.fori_loop(c * span // 8, (c + 1) * span // 8, tile, 0)
        rows = pl.ds(c * span, span)
        copy = pltpu.make_async_copy(obuf.at[:, :, rows, :], out.at[:, :, rows, :], sems.at[c])
        copy.start()
        copies.append(copy)
    for copy in copies:
        copy.wait()


def smem():
    return pl.BlockSpec(memory_space=pltpu.SMEM)


def vmem(n):
    return [pl.BlockSpec(memory_space=VM)] * n


def hbm():
    return pl.BlockSpec(memory_space=pl.ANY)


def near(*values):
    return [pltpu.with_memory_space_constraint(v, VM) for v in values]


def room(mib):
    return pltpu.CompilerParams(vmem_limit_bytes=mib * 1024 * 1024)


def ring(size, step):
    return [(i, (i + step) % size) for i in range(size)]


def on_device(field, source):
    gx = lax.axis_index("gx")
    flip = (gx % 2).astype(jnp.int32)[None]
    last = lax.axis_size("gx") - 1
    wall = jnp.where((gx == 0) | (gx == last), 0.0, SIXTH).astype(F32)[None]
    pairs = lax.axis_size("gx") // 2
    chip = [p for i in range(pairs) for p in ((2 * i, 2 * i + 1), (2 * i + 1, 2 * i))]
    across = [p for i in range(pairs - 1) for p in ((2 * i + 1, 2 * i + 2), (2 * i + 2, 2 * i + 1))]
    ny, nz = lax.axis_size("gy"), lax.axis_size("gz")

    fields, sources = [
        pltpu.with_memory_space_constraint(a.reshape(Q, 2, NY, NZ), pltpu.HBM) for a in (field, source)
    ]
    work = VM((Q, ROWS, NZ), F32)
    face = VM((Q, NY, NZ), F32)
    bm, srm, sbm, high, low, zlow, zhigh = pl.pallas_call(
        pack_kernel,
        name="pack", compiler_params=room(8),
        out_shape=(work, work, work, face, face, VM((NY, NZ), F32), VM((NY, NZ), F32)),
        in_specs=[smem(), hbm(), hbm()],
        out_specs=vmem(7),
        scratch_shapes=[VM((Q, 2, NY, NZ), F32), VM((Q, 2, NY, NZ), F32), pltpu.SemaphoreType.DMA((2 * CHUNKS,))],
    )(flip, fields, sources)

    high = lax.ppermute(high, "gx", chip)
    low = lax.ppermute(low, "gx", across)
    zr = lax.ppermute(zlow, "gz", ring(nz, -1))
    zl = lax.ppermute(zhigh, "gz", ring(nz, 1))
    bm, srm, sbm, zr, zl = near(bm, srm, sbm, zr, zl)
    strip = VM((26, 8, NZ), F32)
    ylow, yhigh = pl.pallas_call(
        y_kernel, name="yfaces", compiler_params=room(2), out_shape=(strip, strip), in_specs=vmem(5), out_specs=vmem(2)
    )(bm, srm, sbm, zr, zl)
    yr = lax.ppermute(ylow, "gy", ring(ny, -1))
    yl = lax.ppermute(yhigh, "gy", ring(ny, 1))
    yr, yl = near(yr, yl)
    corner = VM((50, 8, NZ), F32)
    chigh, clow = pl.pallas_call(
        corner_kernel, name="corners", compiler_params=room(2), out_shape=(corner, corner), in_specs=vmem(4), out_specs=vmem(2)
    )(yr, yl, zr, zl)
    chigh = lax.ppermute(chigh, "gx", chip)
    clow = lax.ppermute(clow, "gx", across)

    zr, zl, yr, yl = near(zr, zl, yr, yl)
    bm, rm, srm, sbm, bh, rh, srh, sbh = pl.pallas_call(
        inner_kernel,
        name="inner", compiler_params=room(4),
        out_shape=(work,) * 8,
        in_specs=[smem()] + vmem(7),
        out_specs=vmem(8),
        input_output_aliases={1: 0, 2: 2, 3: 3},
    )(flip, bm, srm, sbm, yr, yl, zr, zl)

    args = near(bm, rm, srm, sbm, bh, rh, srh, sbh, high, low, chigh, clow)
    halo3, halo2 = VM((6, ROWS, NZ), F32), VM((4, ROWS, NZ), F32)
    out = pl.pallas_call(
        outer_kernel,
        name="outer", compiler_params=room(16),
        out_shape=(jax.ShapeDtypeStruct((Q, 2, NY, NZ), F32),) + (work,) * 4,
        in_specs=[smem(), smem()] + vmem(12),
        out_specs=[hbm()] + vmem(4),
        input_output_aliases={2: 1, 3: 2, 6: 3, 7: 4},
        scratch_shapes=[halo3] * 6 + [halo2] * 2 + [VM((Q, 2, NY, NZ), F32), pltpu.SemaphoreType.DMA((OUT_CHUNKS,))],
    )(flip, wall, *args)[0]
    return out.reshape(field.shape)


def solution(mesh):
    spec = P("gx", "gy", "gz")
    return jax.shard_map(on_device, mesh=mesh, in_specs=(spec, spec), out_specs=spec, check_vma=False)
```

profile of v0, /device:TPU:1, one launch (start us, length us, event | category | flops | bytes accessed | tf_op | source)
XLA Modules:
  0.0 104.5 jit_solution(8231534411436078908)
XLA Ops:
  0.0 6.0 %pack.1 = (f32[8,288,128]{2,1,0:T(8,128)S(1)}, f32[8,288,128]{2,1,0:T(8,128)S(1)}, f32[8,288,128]{2,1,0:T(8,128)S(1)}, f32[8,256,128]{2,1,0:T(8,128)}, f32[8,256...) custom-call(s32[1]{0:T(128)} %bitcast.flip_ref, f32[8,2,256,128]{3,2,1,0:T(8,128)} %bitcast.5, ...), custom_call_target="tpu_custom_call" | custom-call | tf_op jit(solution)/shard_map/pack/pallas_call | solution.py:370
  6.0 1.5 %collective-permute-start.4 = (f32[8,256,128]{2,1,0:T(8,128)}, f32[8,256,128]{2,1,0:T(8,128)}, u32[]{:S(2)}, u32[]{:S(2)}) collective-permute-start(f32[8,256,128]{2,1,0:T(8,128)} %get-tuple-element.40), channel_id=1, source_target_pairs={{0,32},{32,0},{64,96},{96,64},{1,33},{33,1},{65,97},{97,65},{2,34}... | collective-permute-start | bytes 3145736 | tf_op jit(solution)/shard_map/ppermute | solution.py:379
  7.4 4.7 %collective-permute-start.5 = (f32[8,256,128]{2,1,0:T(8,128)}, f32[8,256,128]{2,1,0:T(8,128)}, u32[]{:S(2)}, u32[]{:S(2)}) collective-permute-start(f32[8,256,128]{2,1,0:T(8,128)} %get-tuple-element.41), channel_id=1, source_target_pairs={{32,64},{64,32},{33,65},{65,33},{34,66},{66,34},{35,67},{67,35},{3... | collective-permute-start | bytes 3145736 | tf_op jit(solution)/shard_map/ppermute | solution.py:380
  12.1 3.9 %collective-permute-start = (f32[256,128]{1,0:T(8,128)S(1)}, f32[256,128]{1,0:T(8,128)S(1)}, u32[]{:S(2)}, u32[]{:S(2)}) collective-permute-start(f32[256,128]{1,0:T(8,128)S(1)} %get-tuple-element.28), channel_id=1, source_target_pairs={{0,7},{1,0},{2,1},{3,2},{4,3},{5,4},{6,5},{7,6},{8,15},{9,8},{10,9... | collective-permute-start | bytes 393224 | tf_op jit(solution)/shard_map/ppermute | solution.py:381
  15.9 0.0 collective-permute-start.1
  16.0 12.3 %collective-permute-done.zr = f32[256,128]{1,0:T(8,128)S(1)} collective-permute-done((f32[256,128]{1,0:T(8,128)S(1)}, f32[256,128]{1,0:T(8,128)S(1)}, u32[]{:S(2)}, u32[]{:S(2)}) %collective-permute-start) | collective-permute-done | bytes 131104 | tf_op jit(solution)/shard_map/ppermute | solution.py:381
  28.2 0.0 copy-start
  28.2 4.2 %collective-permute-done.1.zl = f32[256,128]{1,0:T(8,128)S(1)} collective-permute-done((f32[256,128]{1,0:T(8,128)S(1)}, f32[256,128]{1,0:T(8,128)S(1)}, u32[]{:S(2)}, u32[]{:S(2)}) %collective-permute-start.1) | collective-permute-done | bytes 131104 | tf_op jit(solution)/shard_map/ppermute | solution.py:382
  32.5 0.0 copy-start.2
  32.5 2.8 %collective-permute-start.2 = (f32[26,8,128]{2,1,0:T(8,128)S(1)}, f32[26,8,128]{2,1,0:T(8,128)S(1)}, u32[]{:S(2)}, u32[]{:S(2)}) collective-permute-start(f32[26,8,128]{2,1,0:T(8,128)S(1)} %get-tuple-element.30), channel_id=1, source_target_pairs={{0,24},{8,0},{16,8},{24,16},{1,25},{9,1},{17,9},{25,17},{2,26},{10... | collective-permute-start | bytes 319496 | tf_op jit(solution)/shard_map/ppermute | solution.py:388
  35.3 0.0 collective-permute-start.3
  35.3 1.7 %collective-permute-done.2.yr = f32[26,8,128]{2,1,0:T(8,128)S(1)} collective-permute-done((f32[26,8,128]{2,1,0:T(8,128)S(1)}, f32[26,8,128]{2,1,0:T(8,128)S(1)}, u32[]{:S(2)}, u32[]{:S(2)}) %collective-permute-start.2) | collective-permute-done | bytes 106528 | tf_op jit(solution)/shard_map/ppermute | solution.py:388
  37.0 0.0 copy-start.4
  37.0 3.0 %collective-permute-done.3.yl = f32[26,8,128]{2,1,0:T(8,128)S(1)} collective-permute-done((f32[26,8,128]{2,1,0:T(8,128)S(1)}, f32[26,8,128]{2,1,0:T(8,128)S(1)}, u32[]{:S(2)}, u32[]{:S(2)}) %collective-permute-start.3) | collective-permute-done | bytes 106528 | tf_op jit(solution)/shard_map/ppermute | solution.py:389
  40.1 0.0 copy-done
  40.1 0.0 copy-done.2
  40.1 3.1 %corners.1 = (f32[50,8,128]{2,1,0:T(8,128)}, f32[50,8,128]{2,1,0:T(8,128)}) custom-call(f32[26,8,128]{2,1,0:T(8,128)S(1)} %collective-permute-done.2.yr, f32[26,8,128]{2,1,0:T(8,128)S(1)} %collective-permute-done.3.yl, f32[256,128]{1,0:T(8,128)S(1)} %collective-permute-done.zr, f32[256,128]{1,0:T(8,128)S(1)} %collective-permute-done.1.zl), custom_call_target="tpu_custom_call" | custom-call | tf_op jit(solution)/shard_map/corners/pallas_call | solution.py:392
  43.2 0.0 copy-done.4
  43.2 0.0 copy-done.6
  43.2 0.0 collective-permute-start.6
  43.2 6.3 %collective-permute-start.7 = (f32[50,8,128]{2,1,0:T(8,128)}, f32[50,8,128]{2,1,0:T(8,128)}, u32[]{:S(2)}, u32[]{:S(2)}) collective-permute-start(f32[50,8,128]{2,1,0:T(8,128)} %get-tuple-element.43), channel_id=1, source_target_pairs={{32,64},{64,32},{33,65},{65,33},{34,66},{66,34},{35,67},{67,35},{3... | collective-permute-start | bytes 614408 | tf_op jit(solution)/shard_map/ppermute | solution.py:396
  49.5 0.0 copy-start.1
  49.5 0.9 copy-done.1
  50.4 0.9 copy-done.3
  51.3 0.9 copy-done.5
  52.2 0.9 copy-done.7
  53.1 23.7 %inner.1 = (f32[8,288,128]{2,1,0:T(8,128)S(1)}, f32[8,288,128]{2,1,0:T(8,128)S(1)}, f32[8,288,128]{2,1,0:T(8,128)S(1)}, f32[8,288,128]{2,1,0:T(8,128)S(1)}, f32[...) custom-call(s32[1]{0:T(128)} %bitcast.flip_ref, ...), custom_call_target="tpu_custom_call", output_to_operand_aliasing={{0}: (1, {}), {2}: (2, {}), {3}: (3, {})} | custom-call | tf_op jit(solution)/shard_map/inner/pallas_call | solution.py:399
  76.8 0.0 collective-permute-done.6.chigh
  76.8 0.0 collective-permute-done.7.clow
  76.8 0.0 collective-permute-done.4.high
  76.8 0.0 collective-permute-done.5.low
  76.8 27.6 %outer.1 = (f32[8,2,256,128]{3,2,1,0:T(8,128)}, f32[8,288,128]{2,1,0:T(8,128)S(1)}, f32[8,288,128]{2,1,0:T(8,128)S(1)}, f32[8,288,128]{2,1,0:T(8,128)S(1)}, f32[8,288,128]{2,1,0:T(8,128)S(1)}) custom-call(s32[1]{0:T(128)} %bitcast.flip_ref, f32[1]{0:T(128)} %bitcast.1.wall_ref, ...), custom_call_target="tpu_custom_call", output_to_operand_aliasing={{1}: (2, {}), {2}: (3, {}), {3}: (6, {}), {4}: (7, {})} | custom-call | tf_op jit(solution)/shard_map/outer/pallas_call | solution.py:410
  (5 shorter events, 0.0 us)
Async XLA Ops:
  6.0 70.9 %collective-permute-start.4 = (f32[8,256,128]{2,1,0:T(8,128)}, f32[8,256,128]{2,1,0:T(8,128)}, u32[]{:S(2)}, u32[]{:S(2)}) collective-permute-start(f32[8,256,128]{2,1,0:T(8,128)} %get-tuple-element.40), channel_id=1, source_target_pairs={{0,32},{32,0},{64,96},{96,64},{1,33},{33,1},{65,97},{97,65},{2,34}... | collective-permute-start | bytes 3145736 | tf_op jit(solution)/shard_map/ppermute | solution.py:379
  7.4 69.4 %collective-permute-start.5 = (f32[8,256,128]{2,1,0:T(8,128)}, f32[8,256,128]{2,1,0:T(8,128)}, u32[]{:S(2)}, u32[]{:S(2)}) collective-permute-start(f32[8,256,128]{2,1,0:T(8,128)} %get-tuple-element.41), channel_id=1, source_target_pairs={{32,64},{64,32},{33,65},{65,33},{34,66},{66,34},{35,67},{67,35},{3... | collective-permute-start | bytes 3145736 | tf_op jit(solution)/shard_map/ppermute | solution.py:380
  12.1 16.1 %collective-permute-start = (f32[256,128]{1,0:T(8,128)S(1)}, f32[256,128]{1,0:T(8,128)S(1)}, u32[]{:S(2)}, u32[]{:S(2)}) collective-permute-start(f32[256,128]{1,0:T(8,128)S(1)} %get-tuple-element.28), channel_id=1, source_target_pairs={{0,7},{1,0},{2,1},{3,2},{4,3},{5,4},{6,5},{7,6},{8,15},{9,8},{10,9... | collective-permute-start | bytes 393224 | tf_op jit(solution)/shard_map/ppermute | solution.py:381
  15.9 16.5 %collective-permute-start.1 = (f32[256,128]{1,0:T(8,128)S(1)}, f32[256,128]{1,0:T(8,128)S(1)}, u32[]{:S(2)}, u32[]{:S(2)}) collective-permute-start(f32[256,128]{1,0:T(8,128)S(1)} %get-tuple-element.29), channel_id=1, source_target_pairs={{0,1},{1,2},{2,3},{3,4},{4,5},{5,6},{6,7},{7,0},{8,9},{9,10},{10,1... | collective-permute-start | bytes 393224 | tf_op jit(solution)/shard_map/ppermute | solution.py:382
  28.2 11.8 %copy-start = (f32[256,128]{1,0:T(8,128)}, f32[256,128]{1,0:T(8,128)S(1)}, u32[]{:S(2)}) copy-start(f32[256,128]{1,0:T(8,128)S(1)} %collective-permute-done.zr) | copy-start | bytes 393220
  32.5 7.6 %copy-start.2 = (f32[256,128]{1,0:T(8,128)}, f32[256,128]{1,0:T(8,128)S(1)}, u32[]{:S(2)}) copy-start(f32[256,128]{1,0:T(8,128)S(1)} %collective-permute-done.1.zl) | copy-start | bytes 393220
  32.5 4.5 %collective-permute-start.2 = (f32[26,8,128]{2,1,0:T(8,128)S(1)}, f32[26,8,128]{2,1,0:T(8,128)S(1)}, u32[]{:S(2)}, u32[]{:S(2)}) collective-permute-start(f32[26,8,128]{2,1,0:T(8,128)S(1)} %get-tuple-element.30), channel_id=1, source_target_pairs={{0,24},{8,0},{16,8},{24,16},{1,25},{9,1},{17,9},{25,17},{2,26},{10... | collective-permute-start | bytes 319496 | tf_op jit(solution)/shard_map/ppermute | solution.py:388
  35.3 4.8 %collective-permute-start.3 = (f32[26,8,128]{2,1,0:T(8,128)S(1)}, f32[26,8,128]{2,1,0:T(8,128)S(1)}, u32[]{:S(2)}, u32[]{:S(2)}) collective-permute-start(f32[26,8,128]{2,1,0:T(8,128)S(1)} %get-tuple-element.31), channel_id=1, source_target_pairs={{0,8},{8,16},{16,24},{24,0},{1,9},{9,17},{17,25},{25,1},{2,10},{10... | collective-permute-start | bytes 319496 | tf_op jit(solution)/shard_map/ppermute | solution.py:389
  37.0 6.2 %copy-start.4 = (f32[26,8,128]{2,1,0:T(8,128)}, f32[26,8,128]{2,1,0:T(8,128)S(1)}, u32[]{:S(2)}) copy-start(f32[26,8,128]{2,1,0:T(8,128)S(1)} %collective-permute-done.2.yr) | copy-start | bytes 319492
  40.1 3.1 %copy-start.6 = (f32[26,8,128]{2,1,0:T(8,128)}, f32[26,8,128]{2,1,0:T(8,128)S(1)}, u32[]{:S(2)}) copy-start(f32[26,8,128]{2,1,0:T(8,128)S(1)} %collective-permute-done.3.yl) | copy-start | bytes 319492
  43.2 33.6 %collective-permute-start.6 = (f32[50,8,128]{2,1,0:T(8,128)}, f32[50,8,128]{2,1,0:T(8,128)}, u32[]{:S(2)}, u32[]{:S(2)}) collective-permute-start(f32[50,8,128]{2,1,0:T(8,128)} %get-tuple-element.42), channel_id=1, source_target_pairs={{0,32},{32,0},{64,96},{96,64},{1,33},{33,1},{65,97},{97,65},{2,34}... | collective-permute-start | bytes 614408 | tf_op jit(solution)/shard_map/ppermute | solution.py:395
  43.2 33.6 %collective-permute-start.7 = (f32[50,8,128]{2,1,0:T(8,128)}, f32[50,8,128]{2,1,0:T(8,128)}, u32[]{:S(2)}, u32[]{:S(2)}) collective-permute-start(f32[50,8,128]{2,1,0:T(8,128)} %get-tuple-element.43), channel_id=1, source_target_pairs={{32,64},{64,32},{33,65},{65,33},{34,66},{66,34},{35,67},{67,35},{3... | collective-permute-start | bytes 614408 | tf_op jit(solution)/shard_map/ppermute | solution.py:396
  49.5 0.9 copy-start.1
  50.4 0.9 copy-start.3
  51.3 0.9 copy-start.5
  52.2 0.9 copy-start.7
where the time goes:
time: 105 us; the launch traced here: 104 us
  Pallas kernels  60.4 us (58%)
  waiting for transfers between devices  21.3 us (20%)
  starting transfers between devices  19.1 us (18%)
  local copies, waits for them, and re-layouts  3.61 us (3%)
    pallas_call x1, Pallas kernels, on_device(): pl.pallas_call(outer_kernel, name='outer', compiler_params=room(16), out_...  27.6 us
    pallas_call x1, Pallas kernels, on_device(): pl.pallas_call(inner_kernel, name='inner', compiler_params=room(4), out_s...  23.7 us
    ppermute x1, waiting for transfers between devices, on_device(): zr = lax.ppermute(zlow, 'gz', ring(nz, -1))  12.3 us
    ppermute x1, starting transfers between devices, on_device(): clow = lax.ppermute(clow, 'gx', across)  6.31 us
    pallas_call x1, Pallas kernels, on_device(): pl.pallas_call(pack_kernel, name='pack', compiler_params=room(8), out_sha...  5.95 us
    ppermute x1, starting transfers between devices, on_device(): low = lax.ppermute(low, 'gx', across)  4.66 us
    ppermute x1, waiting for transfers between devices, on_device(): zl = lax.ppermute(zhigh, 'gz', ring(nz, 1))  4.22 us
    ppermute x1, starting transfers between devices, on_device(): zr = lax.ppermute(zlow, 'gz', ring(nz, -1))  3.85 us
  transfers between devices with their start and end apart: 8, of which 4 were waited for; matrix products, arithmetic and copies ran while one was open for 0% of the time, Pallas kernels for 26%

commit v1 on v0

v1 whole, which is shorter than its diff:
```python
import jax
import jax.numpy as jnp
from jax import lax
from jax.experimental import pallas as pl
from jax.experimental.pallas import tpu as pltpu
from jax.sharding import PartitionSpec as P


F32 = jnp.float32
VM = pltpu.VMEM
Q, NY, NZ = 8, 256, 128
ROWS = NY + 32
TILES = NY // 8
SIXTH = 1.0 / 6.0


def lanes_of():
    return lax.broadcasted_iota(jnp.int32, (8, 128), 1)


def odd_cells():
    return (lax.broadcasted_iota(jnp.int32, (8, 128), 0) + lanes_of()) % 2


def turn(value, shift):
    shift = shift % 128
    return value if shift == 0 else pltpu.roll(value, shift, 1)


def mirrored(q, flip):
    return q + flip * (Q - 1 - 2 * q)


BATCH = 40


def batched(count, size, body):
    def step(i, carry):
        body(i * size, size)
        return carry

    lax.fori_loop(0, count // size, step, 0)
    if count % size:
        body(count - count % size, count % size)


CHUNKS = 4


def pack_kernel(flip_ref, field, source, bm, srm, sbm, zlow, zhigh, fbuf, sbuf, sems):
    flip = flip_ref[0] % 2
    span = NY // CHUNKS
    copies = []
    for c in range(CHUNKS):
        rows = pl.ds(c * span, span)
        for n, (src, dst) in enumerate(((field, fbuf), (source, sbuf))):
            copy = pltpu.make_async_copy(src.at[:, :, rows, :], dst.at[:, :, rows, :], sems.at[2 * c + n])
            copy.start()
            copies.append(copy)
    odd = odd_cells() == 1
    lane = lanes_of()
    col = lane % 16
    left_half = lane < 64

    def tile(t):
        r = pl.multiple_of(t * 8, 8)
        rows = pl.ds(r, 8)
        put = pl.ds(pl.multiple_of(r + 16, 8), 8)
        acc = [jnp.zeros((8, 128), F32)] * 4
        for q in range(Q):
            at = mirrored(q, flip)
            f0, f1 = fbuf[at, 0, rows, :], fbuf[at, 1, rows, :]
            s0, s1 = sbuf[at, 0, rows, :], sbuf[at, 1, rows, :]
            b = jnp.where(odd, f0, f1)
            sr = jnp.where(odd, s1, s0)
            sb = jnp.where(odd, s0, s1)
            bm[q, put, :] = b
            srm[q, put, :] = sr
            sbm[q, put, :] = sb
            here = lane // 16 == q
            parts = (
                turn(b, 16 * q),
                turn(jnp.where(left_half, sr, b), 16 * q + 6),
                turn(jnp.where(left_half, sb, sr), 16 * q + 11),
                turn(sb, 16 * q + 15),
            )
            acc = [jnp.where(here, new, old) for new, old in zip(parts, acc)]
        zlow[rows, :] = jnp.where(col < 6, acc[0], jnp.where(col < 11, acc[1], acc[2]))
        zhigh[rows, :] = jnp.where(col < 6, acc[1], jnp.where(col < 11, acc[2], acc[3]))

    def body(i, carry):
        for u in range(4):
            tile(i * 4 + u)
        return carry

    for c in range(CHUNKS):
        copies[2 * c].wait()
        copies[2 * c + 1].wait()
        lax.fori_loop(c * span // 32, (c + 1) * span // 32, body, 0)


def face_kernel(bm, srm, sbm, high, low):
    def body(i, carry):
        rows = pl.ds(pl.multiple_of(i * 32, 32), 32)
        put = pl.ds(pl.multiple_of(i * 32 + 16, 16), 32)
        for out, planes in ((low, (0, 1, 2)), (high, (7, 6, 5))):
            for d, q in enumerate(planes):
                out[d, rows, :] = bm[q, put, :]
                out[3 + d, rows, :] = srm[q, put, :]
                if d < 2:
                    out[6 + d, rows, :] = sbm[q, put, :]
        return carry

    lax.fori_loop(0, NY // 32, body, 0)


def y_kernel(bm, srm, sbm, zr, zl, ylow, yhigh):
    for out, row in ((ylow, 0), (yhigh, NY - 8)):
        for n, ref in enumerate((bm, srm, sbm)):
            for q in range(Q):
                out[8 * n + q] = ref[q, row + 16:row + 24, :]
        out[24] = zr[row:row + 8, :]
        out[25] = zl[row:row + 8, :]


def put_rim(rows, r, l, bh, srh, sbh):
    lane = lanes_of()
    col = lane % 16
    one = jnp.where(col < 6, l, r)
    two = jnp.where(col < 11, l, r)
    for q in range(Q):
        parts = [turn(r, -16 * q), turn(one, -16 * q - 6), turn(two, -16 * q - 11), turn(l, 113 - 16 * q)]
        for n, (ref, width) in enumerate(((bh, 6), (srh, 5), (sbh, 4))):
            ref[q, rows, :] = jnp.where(lane < width, parts[n], jnp.where(lane >= 128 - width, parts[n + 1], 0.0))


def rim_kernel(zr, zl, bh, srh, sbh):
    def body(first, tiles):
        for u in range(tiles):
            r = pl.multiple_of((first + u) * 8, 8)
            put_rim(pl.ds(pl.multiple_of(r + 16, 8), 8), zr[pl.ds(r, 8), :], zl[pl.ds(r, 8), :], bh, srh, sbh)

    batched(TILES, 4, body)


def corner_kernel(yr, yl, zr, zl, bm_in, srm_in, sbm_in, bh_in, srh_in, sbh_in, high, low, bm, srm, sbm, bh, srh, sbh):
    del bm_in, srm_in, sbm_in, bh_in, srh_in, sbh_in
    lane = lanes_of()
    left_half = lane < 64
    for out, planes in ((low, (0, 1, 2)), (high, (7, 6, 5))):
        for side, ref in enumerate((yr, yl)):
            for d, q in enumerate(planes):
                out[8 * side + d] = ref[q]
                out[8 * side + 3 + d] = ref[8 + q]
                if d < 2:
                    out[8 * side + 6 + d] = ref[16 + q]

    def put(n, r, l):
        low[n] = jnp.where(left_half, r, turn(l, 64))
        high[n] = jnp.where(left_half, turn(r, 48), turn(l, 112))

    def body(first, tiles):
        for u in range(tiles):
            rows = pl.ds(pl.multiple_of((first + u) * 8, 8), 8)
            put(first + u + 17, zr[rows, :], zl[rows, :])

    put(16, yl[24], yl[25])
    put(49, yr[24], yr[25])
    batched(TILES, 16, body)
    for row, ref in ((8, yl), (NY + 16, yr)):
        for q in range(Q):
            bm[q, row:row + 8, :] = ref[q]
            srm[q, row:row + 8, :] = ref[8 + q]
            sbm[q, row:row + 8, :] = ref[16 + q]
        put_rim(pl.ds(row, 8), ref[24], ref[25], bh, srh, sbh)


def mirror_jobs(jobs):
    swap = {"both": "both", "up": "down", "down": "up"}
    return [(Q - 1 - q, swap[x], None if keep is None else 1 - keep) for q, x, keep in jobs]


def half_sweep(r, red, jobs, odd, lane, get, factor, rims=True):
    first, last = lane == 0, lane == 127
    rows = pl.ds(r, 8)
    above, below = pl.ds(r - 1, 8), pl.ds(r + 1, 8)
    centre = {}

    def at(q):
        if q not in centre:
            main, rim = get("black" if red else "red", q)
            centre[q] = (main[rows, :], rim[rows, :] if rims else None)
        return centre[q]

    done = {}
    for q, x, keep in jobs:
        mains = get("black" if red else "red", q)
        sources = get("sr" if red else "sb", q)
        olds = get("red" if red else "black", q)
        cm = at(q)[0]
        ch = at(q)[1] if rims else mains[1][rows, :]
        lm, lh = turn(cm, 1), turn(ch, 1)
        rm, rh = turn(cm, 127), turn(ch, 127)
        beside = (
            jnp.where(first, lh, lm) + jnp.where(last, rh, rm),
            jnp.where(first, lm, lh) + jnp.where(last, rm, rh) if rims else None,
        )
        new = []
        for n in range(2 if rims else 1):
            if x == "up":
                along = at(q + 1)[n]
            elif x == "down":
                along = at(q - 1)[n]
            elif red:
                along = jnp.where(odd, at(q + 1)[n], at(q - 1)[n])
            else:
                along = jnp.where(odd, at(q - 1)[n], at(q + 1)[n])
            total = (sources[n][rows, :] + at(q)[n]) + (along + beside[n])
            total = total + (mains[n][above, :] + mains[n][below, :])
            value = total * factor(q)
            if keep == 1:
                value = jnp.where(odd, olds[n][rows, :], value)
            elif keep == 0:
                value = jnp.where(odd, value, olds[n][rows, :])
            new.append(value)
        done[q] = new
    return done


def sweep_rows(red, jobs, odd, lane, get, factor):
    def body(first, tiles):
        fresh = []
        for u in range(tiles):
            r = pl.multiple_of((first + u) * 8 + 8, 8)
            fresh.append((r, half_sweep(r, red, jobs, odd, lane, get, factor)))
        for r, done in fresh:
            for q, new in done.items():
                for ref, value in zip(get("red" if red else "black", q), new):
                    ref[pl.ds(r, 8), :] = value

    batched(TILES + 2, max(1, BATCH // len(jobs)), body)


def full(*qs):
    return [(q, "both", None) for q in qs]


def inner_kernel(flip_ref, bm_in, srm, sbm, bh_in, srh, sbh, bm, rm, bh, rh):
    del bm_in, bh_in
    lane = lanes_of()
    odd = (odd_cells() + flip_ref[0] % 2) % 2 == 1

    table = {"black": (bm, bh), "red": (rm, rh), "sr": (srm, srh), "sb": (sbm, sbh)}

    def get(kind, q):
        return [ref.at[q] for ref in table[kind]]

    def factor(q):
        return SIXTH

    edge1, edge3, edge5 = [(0, "up", None)], [(1, "up", 0)], [(2, "up", 0)]
    for red, jobs in (
        (True, edge1 + full(*range(1, 7)) + mirror_jobs(edge1)),
        (False, full(*range(1, 7))),
        (True, edge3 + full(*range(2, 6)) + mirror_jobs(edge3)),
        (False, full(*range(2, 6))),
        (True, edge5 + full(3, 4) + mirror_jobs(edge5)),
        (False, full(3, 4)),
    ):
        sweep_rows(red, jobs, odd, lane, get, factor)


OUT_CHUNKS = 4


def outer_kernel(flip_ref, bm_in, rm_in, srm, sbm, bh_in, rh_in, srh, sbh, high, low, chigh, clow,
                 out, bm, rm, bh, rh, xbm, xbh, xrm, xrh, xsrm, xsrh, xsbm, xsbh, obuf, sems):
    del bm_in, rm_in, bh_in, rh_in
    flip = flip_ref[0] % 2
    wall = jnp.where(flip_ref[0] >= 2, 0.0, SIXTH)
    lane = lanes_of()
    plain = odd_cells() == 1
    odd = (odd_cells() + flip) % 2 == 1

    for side, main, corner in ((0, low, clow), (1, high, chigh)):
        for d in range(3):
            for n, (ref, deep) in enumerate(((xbm, 3), (xsrm, 3), (xsbm, 2))):
                if d < deep:
                    slot_n = deep * side + d
                    ref[slot_n, 8:16, :] = corner[8 + 3 * n + d]
                    ref[slot_n, 16:NY + 16, :] = main[3 * n + d]
                    ref[slot_n, NY + 16:NY + 24, :] = corner[3 * n + d]

    def rim(first, tiles):
        for u in range(tiles):
            t = first + u
            rows = pl.ds(pl.multiple_of(t * 8 + 8, 8), 8)
            for side, corner in ((0, clow), (1, chigh)):
                both = corner[16 + t]
                for d in range(3):
                    c = 16 * (d if side == 0 else 2 - d)
                    for n, (ref, deep, width) in enumerate(((xbh, 3, 6), (xsrh, 3, 5), (xsbh, 2, 4))):
                        if d < deep:
                            off = c + (0, 6, 11)[n]
                            right = turn(both, -off)
                            left = turn(both, 128 - width - 64 - off)
                            ref[deep * side + d, rows, :] = jnp.where(
                                lane < width, right, jnp.where(lane >= 128 - width, left, 0.0)
                            )

    batched(TILES + 2, 3, rim)

    own = {"black": (bm, bh), "red": (rm, rh), "sr": (srm, srh), "sb": (sbm, sbh)}
    halo = {"black": (xbm, xbh), "red": (xrm, xrh), "sr": (xsrm, xsrh), "sb": (xsbm, xsbh)}

    def get(kind, q):
        if 0 <= q < Q:
            return [ref.at[q] for ref in own[kind]]
        deep = 2 if kind == "sb" else 3
        slot = -1 - q if q < 0 else deep + q - Q
        return [ref.at[slot] for ref in halo[kind]]

    def factor(q):
        return wall if q < 0 else SIXTH

    for red, jobs in (
        (True, [(-3, "up", None)] + full(-2, -1) + [(0, "down", 1)]),
        (False, full(-2, -1, 0)),
        (True, [(-2, "up", None)] + full(-1, 0) + [(1, "down", 1)]),
        (False, full(-1, 0, 1)),
        (True, [(-1, "up", None)] + full(0, 1) + [(2, "down", 1)]),
    ):
        sweep_rows(red, jobs + mirror_jobs(jobs), odd, lane, get, factor)

    jobs = full(0, 1, 2)
    jobs = jobs + mirror_jobs(jobs)

    def tiles(i, carry):
        for u in range(4):
            t = i * 4 + u
            r = pl.multiple_of(t * 8 + 16, 8)
            rows = pl.ds(pl.multiple_of(t * 8, 8), 8)
            new = half_sweep(r, False, jobs, odd, lane, get, factor, rims=False)
            for q in range(Q):
                b = new[q][0] if q in new else bm[q, pl.ds(r, 8), :]
                v = rm[q, pl.ds(r, 8), :]
                at = mirrored(q, flip)
                obuf[at, 0, rows, :] = jnp.where(plain, b, v)
                obuf[at, 1, rows, :] = jnp.where(plain, v, b)
        return carry

    span = NY // OUT_CHUNKS
    copies = []
    for c in range(OUT_CHUNKS):
        lax.fori_loop(c * span // 32, (c + 1) * span // 32, tiles, 0)
        rows = pl.ds(c * span, span)
        copy = pltpu.make_async_copy(obuf.at[:, :, rows, :], out.at[:, :, rows, :], sems.at[c])
        copy.start()
        copies.append(copy)
    for copy in copies:
        copy.wait()


def smem():
    return pl.BlockSpec(memory_space=pltpu.SMEM)


def hbm():
    return pl.BlockSpec(memory_space=pl.ANY)


def near(value):
    return pltpu.with_memory_space_constraint(value, VM)


def room(mib):
    return pltpu.CompilerParams(vmem_limit_bytes=mib * 1024 * 1024)


def ring(size, step):
    return [(i, (i + step) % size) for i in range(size)]


def kernel(body, mib, outs, ins, **more):
    pairs = [i if isinstance(i, tuple) else (near(i), pl.BlockSpec(memory_space=VM)) for i in ins]
    arrays, specs = zip(*pairs)
    out_specs = more.pop("out_specs", [pl.BlockSpec(memory_space=VM)] * len(outs))
    return pl.pallas_call(
        body, out_shape=outs, in_specs=specs, out_specs=out_specs, compiler_params=room(mib), **more
    )(*arrays)


def send(value, axis, pairs):
    return lax.ppermute(near(value), axis, pairs)


def all_sweeps(field, source):
    gx = lax.axis_index("gx")
    last = lax.axis_size("gx") - 1
    walled = (gx == 0) | (gx == last)
    flip = (gx % 2 + 2 * walled.astype(jnp.int32))[None], smem()
    pairs = lax.axis_size("gx") // 2
    chip = [p for i in range(pairs) for p in ((2 * i, 2 * i + 1), (2 * i + 1, 2 * i))]
    across = [p for i in range(pairs - 1) for p in ((2 * i + 1, 2 * i + 2), (2 * i + 2, 2 * i + 1))]
    ny, nz = lax.axis_size("gy"), lax.axis_size("gz")

    blocks = [
        (pltpu.with_memory_space_constraint(a.reshape(Q, 2, NY, NZ), pltpu.HBM), hbm()) for a in (field, source)
    ]
    work, face, block = VM((Q, ROWS, NZ), F32), VM((Q, NY, NZ), F32), VM((Q, 2, NY, NZ), F32)
    rows, strip, corner = VM((NY, NZ), F32), VM((26, 8, NZ), F32), VM((50, 8, NZ), F32)

    bm, srm, sbm, zlow, zhigh = kernel(
        pack_kernel, 8, (work,) * 3 + (rows,) * 2, [flip] + blocks,
        scratch_shapes=[block, block, pltpu.SemaphoreType.DMA((2 * CHUNKS,))],
    )
    zr = send(zlow, "gz", ring(nz, -1))
    zl = send(zhigh, "gz", ring(nz, 1))
    high, low = kernel(face_kernel, 2, (face, face), [bm, srm, sbm])
    high = send(high, "gx", chip)
    low = send(low, "gx", across)
    ylow, yhigh = kernel(y_kernel, 2, (strip, strip), [bm, srm, sbm, zr, zl])
    yr = send(ylow, "gy", ring(ny, -1))
    yl = send(yhigh, "gy", ring(ny, 1))
    bh, srh, sbh = kernel(rim_kernel, 2, (work,) * 3, [zr, zl])
    chigh, clow, bm, srm, sbm, bh, srh, sbh = kernel(
        corner_kernel, 2, (corner, corner) + (work,) * 6, [yr, yl, zr, zl, bm, srm, sbm, bh, srh, sbh],
        input_output_aliases={4 + i: 2 + i for i in range(6)},
    )
    chigh = send(chigh, "gx", chip)
    clow = send(clow, "gx", across)
    bm, rm, bh, rh = kernel(
        inner_kernel, 4, (work,) * 4, [flip, bm, srm, sbm, bh, srh, sbh], input_output_aliases={1: 0, 4: 2}
    )
    halo3, halo2 = VM((6, ROWS, NZ), F32), VM((4, ROWS, NZ), F32)
    out = kernel(
        outer_kernel, 16, (jax.ShapeDtypeStruct((Q, 2, NY, NZ), F32),) + (work,) * 4,
        [flip, bm, rm, srm, sbm, bh, rh, srh, sbh, high, low, chigh, clow],
        out_specs=[hbm()] + [pl.BlockSpec(memory_space=VM)] * 4,
        input_output_aliases={1: 1, 2: 2, 5: 3, 6: 4},
        scratch_shapes=[halo3] * 6 + [halo2] * 2 + [block, pltpu.SemaphoreType.DMA((OUT_CHUNKS,))],
    )[0]
    return out.reshape(field.shape)


def solution(mesh):
    spec = P("gx", "gy", "gz")
    return jax.shard_map(all_sweeps, mesh=mesh, in_specs=(spec, spec), out_specs=spec, check_vma=False)
```

time: 105 us -> 63.2 us (0.60)
  Pallas kernels: 60.4 us -> 24.3 us
  local copies, waits for them, and re-layouts: 3.61 us -> 0 us
  waiting for transfers between devices: 21.3 us -> 19.5 us
    pallas_call x5 -> x7, Pallas kernels: 60.4 us -> 24.3 us  [kernel(): pl.pallas_call(body, out_shape=outs, in_specs=specs, out_specs=out_specs,...]
    unnamed x16 -> x0, local copies, waits for them, and re-layouts: 3.61 us -> none
    ppermute x8, waiting for transfers between devices: 21.3 us -> 19.5 us  [send(): return lax.ppermute(near(value), axis, pairs)]
  transfers between devices with their start and end apart: 8 -> 8, of which waited for: 4 -> 4; matrix products, arithmetic and copies ran while one was open for 0% -> 0% of each run, Pallas kernels for 26% -> 14%
where the time goes in v1:
time: 63.2 us; the launch traced here: 63 us
  Pallas kernels  24.3 us (38%)
  waiting for transfers between devices  19.5 us (31%)
  starting transfers between devices  19.2 us (30%)
    pallas_call x7, Pallas kernels, kernel(): pl.pallas_call(body, out_shape=outs, in_specs=specs, out_specs=out_specs,...  24.3 us
    ppermute x8, waiting for transfers between devices, send(): return lax.ppermute(near(value), axis, pairs)  19.5 us
    ppermute x8, starting transfers between devices, send(): return lax.ppermute(near(value), axis, pairs)  19.2 us
  transfers between devices with their start and end apart: 8, of which 4 were waited for; matrix products, arithmetic and copies ran while one was open for 0% of the time, Pallas kernels for 14%

profile of v1, /device:TPU:1, one launch (start us, length us, event | category | flops | bytes accessed | tf_op | source)
XLA Modules:
  0.0 63.0 jit_solution(7098479175281687446)
XLA Ops:
  0.0 2.9 %shard_map.28 = (f32[8,288,128]{2,1,0:T(8,128)S(1)}, f32[8,288,128]{2,1,0:T(8,128)S(1)}, f32[8,288,128]{2,1,0:T(8,128)S(1)}, f32[256,128]{1,0:T(8,128)S(1)}, f32[256,128]{1,0:T(8,128)S(1)}) custom-call(s32[1]{0:T(128)} %bitcast.flip_ref, f32[8,2,256,128]{3,2,1,0:T(8,128)} %bitcast.4, f32[8,2,256,128]{3,2,1,0:T(8,128)} %bitcast.5), custom_call_target="tpu_custom_call" | custom-call | tf_op jit(solution)/shard_map/pallas_call | solution.py:388
  2.9 0.2 shard_map.33
  3.1 1.5 %collective-permute-start.4 = (f32[8,256,128]{2,1,0:T(8,128)S(1)}, f32[8,256,128]{2,1,0:T(8,128)S(1)}, u32[]{:S(2)}, u32[]{:S(2)}) collective-permute-start(f32[8,256,128]{2,1,0:T(8,128)S(1)} %get-tuple-element.50), channel_id=1, source_target_pairs={{0,32},{32,0},{64,96},{96,64},{1,33},{33,1},{65,97},{97,65},{2,34}... | collective-permute-start | bytes 3145736 | tf_op jit(solution)/shard_map/ppermute | solution.py:394
  4.6 4.7 %collective-permute-start.5 = (f32[8,256,128]{2,1,0:T(8,128)S(1)}, f32[8,256,128]{2,1,0:T(8,128)S(1)}, u32[]{:S(2)}, u32[]{:S(2)}) collective-permute-start(f32[8,256,128]{2,1,0:T(8,128)S(1)} %get-tuple-element.51), channel_id=1, source_target_pairs={{32,64},{64,32},{33,65},{65,33},{34,66},{66,34},{35,67},{67,35},{3... | collective-permute-start | bytes 3145736 | tf_op jit(solution)/shard_map/ppermute | solution.py:394
  9.2 3.9 %collective-permute-start = (f32[256,128]{1,0:T(8,128)S(1)}, f32[256,128]{1,0:T(8,128)S(1)}, u32[]{:S(2)}, u32[]{:S(2)}) collective-permute-start(f32[256,128]{1,0:T(8,128)S(1)} %get-tuple-element.33), channel_id=1, source_target_pairs={{0,7},{1,0},{2,1},{3,2},{4,3},{5,4},{6,5},{7,6},{8,15},{9,8},{10,9... | collective-permute-start | bytes 393224 | tf_op jit(solution)/shard_map/ppermute | solution.py:394
  13.1 0.0 collective-permute-start.1
  13.1 12.1 %collective-permute-done.zr = f32[256,128]{1,0:T(8,128)S(1)} collective-permute-done((f32[256,128]{1,0:T(8,128)S(1)}, f32[256,128]{1,0:T(8,128)S(1)}, u32[]{:S(2)}, u32[]{:S(2)}) %collective-permute-start) | collective-permute-done | bytes 131104 | tf_op jit(solution)/shard_map/ppermute | solution.py:394
  25.2 4.2 %collective-permute-done.1.zl = f32[256,128]{1,0:T(8,128)S(1)} collective-permute-done((f32[256,128]{1,0:T(8,128)S(1)}, f32[256,128]{1,0:T(8,128)S(1)}, u32[]{:S(2)}, u32[]{:S(2)}) %collective-permute-start.1) | collective-permute-done | bytes 131104 | tf_op jit(solution)/shard_map/ppermute | solution.py:394
  29.4 2.8 %collective-permute-start.2 = (f32[26,8,128]{2,1,0:T(8,128)S(1)}, f32[26,8,128]{2,1,0:T(8,128)S(1)}, u32[]{:S(2)}, u32[]{:S(2)}) collective-permute-start(f32[26,8,128]{2,1,0:T(8,128)S(1)} %get-tuple-element.35), channel_id=1, source_target_pairs={{0,24},{8,0},{16,8},{24,16},{1,25},{9,1},{17,9},{25,17},{2,26},{10... | collective-permute-start | bytes 319496 | tf_op jit(solution)/shard_map/ppermute | solution.py:394
  32.2 0.0 collective-permute-start.3
  32.2 1.6 %shard_map.30 = (f32[8,288,128]{2,1,0:T(8,128)S(1)}, f32[8,288,128]{2,1,0:T(8,128)S(1)}, f32[8,288,128]{2,1,0:T(8,128)S(1)}) custom-call(f32[256,128]{1,0:T(8,128)S(1)} %collective-permute-done.zr, f32[256,128]{1,0:T(8,128)S(1)} %collective-permute-done.1.zl), custom_call_target="tpu_custom_call" | custom-call | tf_op jit(solution)/shard_map/pallas_call | solution.py:388
  33.8 0.1 collective-permute-done.2.yr
  33.9 3.0 %collective-permute-done.3.yl = f32[26,8,128]{2,1,0:T(8,128)S(1)} collective-permute-done((f32[26,8,128]{2,1,0:T(8,128)S(1)}, f32[26,8,128]{2,1,0:T(8,128)S(1)}, u32[]{:S(2)}, u32[]{:S(2)}) %collective-permute-start.3) | collective-permute-done | bytes 106528 | tf_op jit(solution)/shard_map/ppermute | solution.py:394
  37.0 0.4 shard_map.31
  37.4 0.1 collective-permute-start.6
  37.5 6.3 %collective-permute-start.7 = (f32[50,8,128]{2,1,0:T(8,128)S(1)}, f32[50,8,128]{2,1,0:T(8,128)S(1)}, u32[]{:S(2)}, u32[]{:S(2)}) collective-permute-start(f32[50,8,128]{2,1,0:T(8,128)S(1)} %get-tuple-element.53), channel_id=1, source_target_pairs={{32,64},{64,32},{33,65},{65,33},{34,66},{66,34},{35,67},{67,35},{3... | collective-permute-start | bytes 614408 | tf_op jit(solution)/shard_map/ppermute | solution.py:394
  43.8 6.8 %shard_map.32 = (f32[8,288,128]{2,1,0:T(8,128)S(1)}, f32[8,288,128]{2,1,0:T(8,128)S(1)}, f32[8,288,128]{2,1,0:T(8,128)S(1)}, f32[8,288,128]{2,1,0:T(8,128)S(1)}) custom-call(s32[1]{0:T(128)} %bitcast.flip_ref, f32[8,288,128]{2,1,0:T(8,128)S(1)} %get-tuple-element.40.bm_in, ...), custom_call_target="tpu_custom_call", output_to_operand_aliasing={{0}: (1, {}), {2}: (4, {})} | custom-call | tf_op jit(solution)/shard_map/pallas_call | solution.py:388
  50.6 0.0 collective-permute-done.6.chigh
  50.6 0.0 collective-permute-done.7.clow
  50.7 0.0 collective-permute-done.4.high
  50.7 0.0 collective-permute-done.5.low
  50.7 12.4 %shard_map.34 = (f32[8,2,256,128]{3,2,1,0:T(8,128)}, f32[8,288,128]{2,1,0:T(8,128)S(1)}, f32[8,288,128]{2,1,0:T(8,128)S(1)}, f32[8,288,128]{2,1,0:T(8,128)S(1)}, f32[8,288,128]{2,1,0:T(8,128)S(1)}) custom-call(s32[1]{0:T(128)} %bitcast.flip_ref, ...), custom_call_target="tpu_custom_call", output_to_operand_aliasing={{1}: (1, {}), {2}: (2, {}), {3}: (5, {}), {4}: (6, {})} | custom-call | tf_op jit(solution)/shard_map/pallas_call | solution.py:388
  (1 shorter events, 0.0 us)
Async XLA Ops:
  3.1 47.6 %collective-permute-start.4 = (f32[8,256,128]{2,1,0:T(8,128)S(1)}, f32[8,256,128]{2,1,0:T(8,128)S(1)}, u32[]{:S(2)}, u32[]{:S(2)}) collective-permute-start(f32[8,256,128]{2,1,0:T(8,128)S(1)} %get-tuple-element.50), channel_id=1, source_target_pairs={{0,32},{32,0},{64,96},{96,64},{1,33},{33,1},{65,97},{97,65},{2,34}... | collective-permute-start | bytes 3145736 | tf_op jit(solution)/shard_map/ppermute | solution.py:394
  4.6 46.1 %collective-permute-start.5 = (f32[8,256,128]{2,1,0:T(8,128)S(1)}, f32[8,256,128]{2,1,0:T(8,128)S(1)}, u32[]{:S(2)}, u32[]{:S(2)}) collective-permute-start(f32[8,256,128]{2,1,0:T(8,128)S(1)} %get-tuple-element.51), channel_id=1, source_target_pairs={{32,64},{64,32},{33,65},{65,33},{34,66},{66,34},{35,67},{67,35},{3... | collective-permute-start | bytes 3145736 | tf_op jit(solution)/shard_map/ppermute | solution.py:394
  9.2 15.9 %collective-permute-start = (f32[256,128]{1,0:T(8,128)S(1)}, f32[256,128]{1,0:T(8,128)S(1)}, u32[]{:S(2)}, u32[]{:S(2)}) collective-permute-start(f32[256,128]{1,0:T(8,128)S(1)} %get-tuple-element.33), channel_id=1, source_target_pairs={{0,7},{1,0},{2,1},{3,2},{4,3},{5,4},{6,5},{7,6},{8,15},{9,8},{10,9... | collective-permute-start | bytes 393224 | tf_op jit(solution)/shard_map/ppermute | solution.py:394
  13.1 16.3 %collective-permute-start.1 = (f32[256,128]{1,0:T(8,128)S(1)}, f32[256,128]{1,0:T(8,128)S(1)}, u32[]{:S(2)}, u32[]{:S(2)}) collective-permute-start(f32[256,128]{1,0:T(8,128)S(1)} %get-tuple-element.34), channel_id=1, source_target_pairs={{0,1},{1,2},{2,3},{3,4},{4,5},{5,6},{6,7},{7,0},{8,9},{9,10},{10,1... | collective-permute-start | bytes 393224 | tf_op jit(solution)/shard_map/ppermute | solution.py:394
  29.4 4.5 %collective-permute-start.2 = (f32[26,8,128]{2,1,0:T(8,128)S(1)}, f32[26,8,128]{2,1,0:T(8,128)S(1)}, u32[]{:S(2)}, u32[]{:S(2)}) collective-permute-start(f32[26,8,128]{2,1,0:T(8,128)S(1)} %get-tuple-element.35), channel_id=1, source_target_pairs={{0,24},{8,0},{16,8},{24,16},{1,25},{9,1},{17,9},{25,17},{2,26},{10... | collective-permute-start | bytes 319496 | tf_op jit(solution)/shard_map/ppermute | solution.py:394
  32.2 4.8 %collective-permute-start.3 = (f32[26,8,128]{2,1,0:T(8,128)S(1)}, f32[26,8,128]{2,1,0:T(8,128)S(1)}, u32[]{:S(2)}, u32[]{:S(2)}) collective-permute-start(f32[26,8,128]{2,1,0:T(8,128)S(1)} %get-tuple-element.36), channel_id=1, source_target_pairs={{0,8},{8,16},{16,24},{24,0},{1,9},{9,17},{17,25},{25,1},{2,10},{10... | collective-permute-start | bytes 319496 | tf_op jit(solution)/shard_map/ppermute | solution.py:394
  37.4 13.2 %collective-permute-start.6 = (f32[50,8,128]{2,1,0:T(8,128)S(1)}, f32[50,8,128]{2,1,0:T(8,128)S(1)}, u32[]{:S(2)}, u32[]{:S(2)}) collective-permute-start(f32[50,8,128]{2,1,0:T(8,128)S(1)} %get-tuple-element.52), channel_id=1, source_target_pairs={{0,32},{32,0},{64,96},{96,64},{1,33},{33,1},{65,97},{97,65},{2,34}... | collective-permute-start | bytes 614408 | tf_op jit(solution)/shard_map/ppermute | solution.py:394
  37.5 13.1 %collective-permute-start.7 = (f32[50,8,128]{2,1,0:T(8,128)S(1)}, f32[50,8,128]{2,1,0:T(8,128)S(1)}, u32[]{:S(2)}, u32[]{:S(2)}) collective-permute-start(f32[50,8,128]{2,1,0:T(8,128)S(1)} %get-tuple-element.53), channel_id=1, source_target_pairs={{32,64},{64,32},{33,65},{65,33},{34,66},{66,34},{35,67},{67,35},{3... | collective-permute-start | bytes 614408 | tf_op jit(solution)/shard_map/ppermute | solution.py:394

commit v2 on v1

v2 whole, which is shorter than its diff:
```python
import jax
import jax.numpy as jnp
from jax import lax
from jax.experimental import pallas as pl
from jax.experimental.pallas import tpu as pltpu
from jax.sharding import PartitionSpec as P


F32 = jnp.float32
VM = pltpu.VMEM
Q, NY, NZ = 8, 256, 128
ROWS = NY + 32
TILES = NY // 8
SIXTH = 1.0 / 6.0


def lanes_of():
    return lax.broadcasted_iota(jnp.int32, (8, 128), 1)


def odd_cells():
    return (lax.broadcasted_iota(jnp.int32, (8, 128), 0) + lanes_of()) % 2


def turn(value, shift):
    shift = shift % 128
    return value if shift == 0 else pltpu.roll(value, shift, 1)


def mirrored(q, flip):
    return q + flip * (Q - 1 - 2 * q)


BATCH = 80


def batched(count, size, body):
    def step(i, carry):
        body(i * size, size)
        return carry

    lax.fori_loop(0, count // size, step, 0)
    if count % size:
        body(count - count % size, count % size)


CHUNKS = 8


def segment(q):
    return q if q < 4 else 11 - q


def split_colours(fbuf, sbuf, at, rows, odd):
    f0, f1 = fbuf[at, 0, rows, :], fbuf[at, 1, rows, :]
    s0, s1 = sbuf[at, 0, rows, :], sbuf[at, 1, rows, :]
    return jnp.where(odd, f0, f1), jnp.where(odd, s1, s0), jnp.where(odd, s0, s1)


def pack_kernel(flip_ref, field, source, fbuf, sbuf, zlow, zhigh, sems):
    flip = flip_ref[0] % 2
    span = NY // CHUNKS
    copies = []
    for c in range(CHUNKS):
        rows = pl.ds(c * span, span)
        for n, (src, dst) in enumerate(((field, fbuf), (source, sbuf))):
            copy = pltpu.make_async_copy(src.at[:, :, rows, :], dst.at[:, :, rows, :], sems.at[2 * c + n])
            copy.start()
            copies.append(copy)
    odd = odd_cells() == 1
    lane = lanes_of()
    col = lane % 16
    left_half = lane < 64

    def tile(t):
        rows = pl.ds(pl.multiple_of(t * 8, 8), 8)
        acc = [jnp.zeros((8, 128), F32)] * 4
        for q in range(Q):
            b, sr, sb = split_colours(fbuf, sbuf, mirrored(q, flip), rows, odd)
            place = 16 * segment(q)
            here = lane // 16 == segment(q)
            parts = (
                turn(b, place),
                turn(jnp.where(left_half, sr, b), place + 6),
                turn(jnp.where(left_half, sb, sr), place + 11),
                turn(sb, place + 15),
            )
            acc = [jnp.where(here, new, old) for new, old in zip(parts, acc)]
        zlow[rows, :] = jnp.where(col < 6, acc[0], jnp.where(col < 11, acc[1], acc[2]))
        zhigh[rows, :] = jnp.where(col < 6, acc[1], jnp.where(col < 11, acc[2], acc[3]))

    for c in range(CHUNKS):
        copies[2 * c].wait()
        copies[2 * c + 1].wait()
        for u in range(span // 8):
            tile(c * span // 8 + u)


def face_kernel(flip_ref, fbuf, sbuf, bm, srm, sbm, high, low):
    flip = flip_ref[0] % 2
    odd = odd_cells() == 1

    def body(first, tiles):
        for u in range(tiles):
            r = pl.multiple_of((first + u) * 8, 8)
            rows = pl.ds(r, 8)
            put = pl.ds(pl.multiple_of(r + 16, 8), 8)
            for q in range(Q):
                values = split_colours(fbuf, sbuf, mirrored(q, flip), rows, odd)
                if q >= 4:
                    values = [turn(v, 64) for v in values]
                for ref, v in zip((bm, srm, sbm), values):
                    ref[q, put, :] = v
                out, d = (low, q) if q < 4 else (high, Q - 1 - q)
                if d < 3:
                    out[d, rows, :] = values[0]
                    out[3 + d, rows, :] = values[1]
                if d < 2:
                    out[6 + d, rows, :] = values[2]

    batched(TILES, 4, body)


def y_kernel(bm, srm, sbm, zr, zl, ylow, yhigh):
    for out, row in ((ylow, 0), (yhigh, NY - 8)):
        for n, ref in enumerate((bm, srm, sbm)):
            for q in range(Q):
                out[8 * n + q] = ref[q, row + 16:row + 24, :]
        out[24] = zr[row:row + 8, :]
        out[25] = zl[row:row + 8, :]


def put_rim(rows, r, l, place, refs):
    lane = lanes_of()
    col, half = lane % 16, lane % 64
    one = jnp.where(col < 6, l, r)
    two = jnp.where(col < 11, l, r)
    parts = [turn(r, -place), turn(one, -place - 6), turn(two, -place - 11), turn(l, -place - 15)]
    for n, (ref, width) in enumerate(zip(refs, (6, 5, 4))):
        ref[rows, :] = jnp.where(half < width, parts[n], jnp.where(half >= 64 - width, parts[n + 1], 0.0))


def rim_kernel(zr, zl, bh, srh, sbh):
    def body(first, tiles):
        for u in range(tiles):
            r = pl.multiple_of((first + u) * 8, 8)
            for a in range(4):
                refs = [ref.at[a] for ref in (bh, srh, sbh)]
                put_rim(pl.ds(pl.multiple_of(r + 16, 8), 8), zr[pl.ds(r, 8), :], zl[pl.ds(r, 8), :], 16 * a, refs)

    batched(TILES, 8, body)


def corner_kernel(yr, yl, zr, zl, bm_in, srm_in, sbm_in, bh_in, srh_in, sbh_in, high, low, bm, srm, sbm, bh, srh, sbh):
    del bm_in, srm_in, sbm_in, bh_in, srh_in, sbh_in
    lane = lanes_of()
    left_half = lane < 64
    for out, planes in ((low, (0, 1, 2)), (high, (7, 6, 5))):
        for side, ref in enumerate((yr, yl)):
            for d, q in enumerate(planes):
                out[8 * side + d] = ref[q]
                out[8 * side + 3 + d] = ref[8 + q]
                if d < 2:
                    out[8 * side + 6 + d] = ref[16 + q]

    def put(n, r, l):
        low[n] = jnp.where(left_half, r, turn(l, 64))
        high[n] = jnp.where(left_half, turn(r, 64), l)

    def body(first, tiles):
        for u in range(tiles):
            rows = pl.ds(pl.multiple_of((first + u) * 8, 8), 8)
            put(first + u + 17, zr[rows, :], zl[rows, :])

    put(16, yl[24], yl[25])
    put(49, yr[24], yr[25])
    batched(TILES, 16, body)
    for row, ref in ((8, yl), (NY + 16, yr)):
        for q in range(Q):
            bm[q, row:row + 8, :] = ref[q]
            srm[q, row:row + 8, :] = ref[8 + q]
            sbm[q, row:row + 8, :] = ref[16 + q]
        for a in range(4):
            put_rim(pl.ds(row, 8), ref[24], ref[25], 16 * a, [rim.at[a] for rim in (bh, srh, sbh)])


class Marks:
    def __init__(self, flip):
        self.lane = lanes_of()
        self.odd = (odd_cells() + flip) % 2 == 1
        turned = (self.lane >= 32) & (self.lane < 96)
        self.rim_odd = self.odd != turned
        self.turned = turned


def half_sweep(r, red, jobs, marks, main, rim, wall, rims=True):
    src, dst, add = ("black", "red", "sr") if red else ("red", "black", "sb")
    lane, odd, rim_odd = marks.lane, marks.odd, marks.rim_odd
    first, last, middle, before = lane == 0, lane == 127, lane == 64, lane == 63
    rows, above, below = pl.ds(r, 8), pl.ds(r - 1, 8), pl.ds(r + 1, 8)
    seen = {}

    def plane(q):
        if q not in seen:
            seen[q] = main(src, q)[rows, :]
        return seen[q]

    def edge(a):
        if ("rim", a) not in seen:
            seen["rim", a] = rim(src, a)[rows, :]
        return seen["rim", a]

    def pick(mark, up, down):
        return jnp.where(mark, up, down) if red else jnp.where(mark, down, up)

    done = {}
    for a, x, keep in jobs:
        b = Q - 1 - a
        turns = [(turn(v, 1), turn(v, 127)) for v in (plane(a), plane(b), edge(a))]
        (l0, r0), (l1, r1), (l2, r2) = turns
        beside = [
            jnp.where(first, l2, l0) + jnp.where(last, r2, r0),
            jnp.where(middle, l2, l1) + jnp.where(before, r2, r1),
        ]
        if rims:
            beside.append(
                jnp.where(first, l0, jnp.where(middle, l1, l2)) + jnp.where(last, r0, jnp.where(before, r1, r2))
            )
        inward = [lambda: plane(a + 1), lambda: plane(b - 1), lambda: edge(a + 1)]
        if a == 3:
            inward = [lambda: turn(plane(4), 64), lambda: turn(plane(3), 64), lambda: turn(edge(3), 64)]
        outward = [lambda: plane(a - 1), lambda: plane(b + 1), lambda: edge(a - 1)]
        refs = [main(src, a), main(src, b), rim(src, a)]
        adds = [main(add, a), main(add, b), rim(add, a)]
        olds = [main(dst, a), main(dst, b), rim(dst, a)]
        new = []
        for n in range(3 if rims else 2):
            if x == "up":
                along = inward[n]()
            elif x == "down":
                along = outward[n]()
            elif n == 1:
                along = pick(odd, outward[n](), inward[n]())
            else:
                along = pick(rim_odd if n == 2 else odd, inward[n](), outward[n]())
            total = (adds[n][rows, :] + (plane(a), plane(b), edge(a))[n]) + (along + beside[n])
            total = total + (refs[n][above, :] + refs[n][below, :])
            value = total * (SIXTH if a >= 0 else wall[n])
            if keep is not None:
                held = [odd, ~odd, rim_odd][n] if keep == 1 else [~odd, odd, ~rim_odd][n]
                value = jnp.where(held, olds[n][rows, :], value)
            new.append(value)
        done[a] = new
    return done


def sweep_rows(red, jobs, marks, main, rim, wall):
    dst = "red" if red else "black"

    def body(first, tiles):
        fresh = []
        for u in range(tiles):
            r = pl.multiple_of((first + u) * 8 + 8, 8)
            fresh.append((r, half_sweep(r, red, jobs, marks, main, rim, wall)))
        for r, done in fresh:
            for a, new in done.items():
                for ref, value in zip((main(dst, a), main(dst, Q - 1 - a), rim(dst, a)), new):
                    ref[pl.ds(r, 8), :] = value

    batched(TILES + 2, max(1, BATCH // len(jobs)), body)


def full(*planes):
    return [(a, "both", None) for a in planes]


def inner_kernel(flip_ref, bm_in, srm, sbm, bh_in, srh, sbh, bm, rm, bh, rh):
    del bm_in, bh_in
    marks = Marks(flip_ref[0] % 2)
    mains = {"black": bm, "red": rm, "sr": srm, "sb": sbm}
    edges = {"black": bh, "red": rh, "sr": srh, "sb": sbh}

    def main(kind, q):
        return mains[kind].at[q]

    def rim(kind, a):
        return edges[kind].at[a]

    for red, jobs in (
        (True, [(0, "up", None)] + full(1, 2, 3)),
        (False, full(1, 2, 3)),
        (True, [(1, "up", 0)] + full(2, 3)),
        (False, full(2, 3)),
        (True, [(2, "up", 0)] + full(3)),
        (False, full(3)),
    ):
        sweep_rows(red, jobs, marks, main, rim, None)


OUT_CHUNKS = 4


def outer_kernel(flip_ref, bm_in, rm_in, srm, sbm, bh_in, rh_in, srh, sbh, high, low, chigh, clow,
                 out, bm, rm, bh, rh, xbm, xbh, xrm, xrh, xsrm, xsrh, xsbm, xsbh, obuf, sems):
    del bm_in, rm_in, bh_in, rh_in
    flip = flip_ref[0] % 2
    marks = Marks(flip)
    lane = marks.lane
    outside = jnp.where(flip_ref[0] >= 2, 0.0, SIXTH)
    wall = (outside, SIXTH, jnp.where(marks.turned, SIXTH, outside))
    plain = odd_cells() == 1

    for side, face, corner in ((0, low, clow), (1, high, chigh)):
        for d in range(3):
            for n, (ref, deep) in enumerate(((xbm, 3), (xsrm, 3), (xsbm, 2))):
                if d < deep:
                    slot = deep * side + d
                    ref[slot, 8:16, :] = corner[8 + 3 * n + d]
                    ref[slot, 16:NY + 16, :] = face[3 * n + d]
                    ref[slot, NY + 16:NY + 24, :] = corner[3 * n + d]

    def fill(first, tiles):
        for u in range(tiles):
            t = first + u
            rows = pl.ds(pl.multiple_of(t * 8 + 8, 8), 8)
            one = clow[16 + t]
            two = turn(chigh[16 + t], 64)
            r = jnp.where(lane < 64, one, two)
            l = turn(jnp.where(lane < 64, two, one), 64)
            for d in range(3):
                put_rim(rows, r, l, 16 * d, [ref.at[d] for ref in (xbh, xsrh, xsbh)[:3 if d < 2 else 2]])

    batched(TILES + 2, 8, fill)

    mains = {"black": (bm, xbm), "red": (rm, xrm), "sr": (srm, xsrm), "sb": (sbm, xsbm)}
    edges = {"black": (bh, xbh), "red": (rh, xrh), "sr": (srh, xsrh), "sb": (sbh, xsbh)}

    def main(kind, q):
        own, halo = mains[kind]
        if 0 <= q < Q:
            return own.at[q]
        return halo.at[-1 - q if q < 0 else (2 if kind == "sb" else 3) + q - Q]

    def rim(kind, a):
        own, halo = edges[kind]
        return own.at[a] if a >= 0 else halo.at[-1 - a]

    for red, jobs in (
        (True, [(-3, "up", None)] + full(-2, -1) + [(0, "down", 1)]),
        (False, full(-2, -1, 0)),
        (True, [(-2, "up", None)] + full(-1, 0) + [(1, "down", 1)]),
        (False, full(-1, 0, 1)),
        (True, [(-1, "up", None)] + full(0, 1) + [(2, "down", 1)]),
    ):
        sweep_rows(red, jobs, marks, main, rim, wall)

    def tiles(i, carry):
        done = []
        for u in range(8):
            t = i * 8 + u
            r = pl.multiple_of(t * 8 + 16, 8)
            done.append((t, r, half_sweep(r, False, full(0, 1, 2), marks, main, rim, wall, rims=False)))
        for t, r, new in done:
            rows = pl.ds(pl.multiple_of(t * 8, 8), 8)
            for q in range(Q):
                a = min(q, Q - 1 - q)
                b = new[a][0 if q == a else 1] if a in new else bm[q, pl.ds(r, 8), :]
                v = rm[q, pl.ds(r, 8), :]
                at = mirrored(q, flip)
                for n, value in enumerate((jnp.where(plain, b, v), jnp.where(plain, v, b))):
                    obuf[at, n, rows, :] = value if q < 4 else turn(value, 64)
        return carry

    span = NY // OUT_CHUNKS
    copies = []
    for c in range(OUT_CHUNKS):
        lax.fori_loop(c * span // 64, (c + 1) * span // 64, tiles, 0)
        rows = pl.ds(c * span, span)
        copy = pltpu.make_async_copy(obuf.at[:, :, rows, :], out.at[:, :, rows, :], sems.at[c])
        copy.start()
        copies.append(copy)
    for copy in copies:
        copy.wait()


def smem():
    return pl.BlockSpec(memory_space=pltpu.SMEM)


def hbm():
    return pl.BlockSpec(memory_space=pl.ANY)


def near(value):
    return pltpu.with_memory_space_constraint(value, VM)


def room(mib):
    return pltpu.CompilerParams(vmem_limit_bytes=mib * 1024 * 1024)


def ring(size, step):
    return [(i, (i + step) % size) for i in range(size)]


def kernel(body, mib, outs, ins, **more):
    pairs = [i if isinstance(i, tuple) else (near(i), pl.BlockSpec(memory_space=VM)) for i in ins]
    arrays, specs = zip(*pairs)
    out_specs = more.pop("out_specs", [pl.BlockSpec(memory_space=VM)] * len(outs))
    return pl.pallas_call(
        body, out_shape=outs, in_specs=specs, out_specs=out_specs, compiler_params=room(mib), **more
    )(*arrays)


def send(value, axis, pairs):
    return lax.ppermute(near(value), axis, pairs)


def all_sweeps(field, source):
    gx = lax.axis_index("gx")
    last = lax.axis_size("gx") - 1
    walled = (gx == 0) | (gx == last)
    flip = (gx % 2 + 2 * walled.astype(jnp.int32))[None], smem()
    pairs = lax.axis_size("gx") // 2
    chip = [p for i in range(pairs) for p in ((2 * i, 2 * i + 1), (2 * i + 1, 2 * i))]
    across = [p for i in range(pairs - 1) for p in ((2 * i + 1, 2 * i + 2), (2 * i + 2, 2 * i + 1))]
    ny, nz = lax.axis_size("gy"), lax.axis_size("gz")

    blocks = [
        (pltpu.with_memory_space_constraint(a.reshape(Q, 2, NY, NZ), pltpu.HBM), hbm()) for a in (field, source)
    ]
    edge = VM((4, ROWS, NZ), F32)
    work, face, block = VM((Q, ROWS, NZ), F32), VM((Q, NY, NZ), F32), VM((Q, 2, NY, NZ), F32)
    rows, strip, corner = VM((NY, NZ), F32), VM((26, 8, NZ), F32), VM((50, 8, NZ), F32)

    fbuf, sbuf, zlow, zhigh = kernel(
        pack_kernel, 2, (block, block, rows, rows), [flip] + blocks,
        scratch_shapes=[pltpu.SemaphoreType.DMA((2 * CHUNKS,))],
    )
    zr = send(zlow, "gz", ring(nz, -1))
    zl = send(zhigh, "gz", ring(nz, 1))
    bm, srm, sbm, high, low = kernel(face_kernel, 2, (work,) * 3 + (face,) * 2, [flip, fbuf, sbuf])
    high = send(high, "gx", chip)
    low = send(low, "gx", across)
    ylow, yhigh = kernel(y_kernel, 2, (strip, strip), [bm, srm, sbm, zr, zl])
    yr = send(ylow, "gy", ring(ny, -1))
    yl = send(yhigh, "gy", ring(ny, 1))
    bh, srh, sbh = kernel(rim_kernel, 2, (edge,) * 3, [zr, zl])
    chigh, clow, bm, srm, sbm, bh, srh, sbh = kernel(
        corner_kernel, 2, (corner, corner) + (work,) * 3 + (edge,) * 3, [yr, yl, zr, zl, bm, srm, sbm, bh, srh, sbh],
        input_output_aliases={4 + i: 2 + i for i in range(6)},
    )
    chigh = send(chigh, "gx", chip)
    clow = send(clow, "gx", across)
    bm, rm, bh, rh = kernel(
        inner_kernel, 4, (work, work, edge, edge), [flip, bm, srm, sbm, bh, srh, sbh], input_output_aliases={1: 0, 4: 2}
    )
    halo = [VM((n, ROWS, NZ), F32) for n in (6, 3, 6, 3, 6, 3, 4, 2)]
    out = kernel(
        outer_kernel, 16, (jax.ShapeDtypeStruct((Q, 2, NY, NZ), F32), work, work, edge, edge),
        [flip, bm, rm, srm, sbm, bh, rh, srh, sbh, high, low, chigh, clow],
        out_specs=[hbm()] + [pl.BlockSpec(memory_space=VM)] * 4,
        input_output_aliases={1: 1, 2: 2, 5: 3, 6: 4},
        scratch_shapes=halo + [block, pltpu.SemaphoreType.DMA((OUT_CHUNKS,))],
    )[0]
    return out.reshape(field.shape)


def solution(mesh):
    spec = P("gx", "gy", "gz")
    return jax.shard_map(all_sweeps, mesh=mesh, in_specs=(spec, spec), out_specs=spec, check_vma=False)
```

time: 63.2 us -> 56.7 us (0.90)
  Pallas kernels: 24.3 us -> 16.6 us
  waiting for transfers between devices: 19.5 us -> 20.3 us
    pallas_call x7, Pallas kernels: 24.3 us -> 16.6 us  [kernel(): pl.pallas_call(body, out_shape=outs, in_specs=specs, out_specs=out_specs,...]
    ppermute x8, waiting for transfers between devices: 19.5 us -> 20.3 us  [send(): return lax.ppermute(near(value), axis, pairs)]
  transfers between devices with their start and end apart: 8 -> 8, of which waited for: 4 -> 4; matrix products, arithmetic and copies ran while one was open for 0% -> 0% of each run, Pallas kernels for 14% -> 9%
where the time goes in v2:
time: 56.7 us; the launch traced here: 56.5 us
  waiting for transfers between devices  20.3 us (36%)
  starting transfers between devices  19.4 us (34%)
  Pallas kernels  16.6 us (29%)
    ppermute x8, waiting for transfers between devices, send(): return lax.ppermute(near(value), axis, pairs)  20.3 us
    ppermute x8, starting transfers between devices, send(): return lax.ppermute(near(value), axis, pairs)  19.4 us
    pallas_call x7, Pallas kernels, kernel(): pl.pallas_call(body, out_shape=outs, in_specs=specs, out_specs=out_specs,...  16.6 us
  transfers between devices with their start and end apart: 8, of which 4 were waited for; matrix products, arithmetic and copies ran while one was open for 0% of the time, Pallas kernels for 9%

profile of v2, /device:TPU:1, one launch (start us, length us, event | category | flops | bytes accessed | tf_op | source)
XLA Modules:
  0.0 56.5 jit_solution(9137910473881411580)
XLA Ops:
  0.0 2.8 %shard_map.28 = (f32[8,2,256,128]{3,2,1,0:T(8,128)S(1)}, f32[8,2,256,128]{3,2,1,0:T(8,128)S(1)}, f32[256,128]{1,0:T(8,128)S(1)}, f32[256,128]{1,0:T(8,128)S(1)}) custom-call(s32[1]{0:T(128)} %bitcast.flip_ref, f32[8,2,256,128]{3,2,1,0:T(8,128)} %bitcast.4, f32[8,2,256,128]{3,2,1,0:T(8,128)} %bitcast.5), custom_call_target="tpu_custom_call" | custom-call | tf_op jit(solution)/shard_map/pallas_call | solution.py:410
  2.8 1.0 %shard_map.29 = (f32[8,288,128]{2,1,0:T(8,128)S(1)}, f32[8,288,128]{2,1,0:T(8,128)S(1)}, f32[8,288,128]{2,1,0:T(8,128)S(1)}, f32[8,256,128]{2,1,0:T(8,128)S(1)}, f32[8,256,128]{2,1,0:T(8,128)S(1)}) custom-call(s32[1]{0:T(128)} %bitcast.flip_ref, f32[8,2,256,128]{3,2,1,0:T(8,128)S(1)} %get-tuple-element.32.fbuf, f32[8,2,256,128]{3,2,1,0:T(8,128)S(1)} %get-tuple-element.33.sbuf), custom_call_target="tpu_custom_call" | custom-call | tf_op jit(solution)/shard_map/pallas_call | solution.py:410
  3.8 1.5 %collective-permute-start.4 = (f32[8,256,128]{2,1,0:T(8,128)S(1)}, f32[8,256,128]{2,1,0:T(8,128)S(1)}, u32[]{:S(2)}, u32[]{:S(2)}) collective-permute-start(f32[8,256,128]{2,1,0:T(8,128)S(1)} %get-tuple-element.54), channel_id=1, source_target_pairs={{0,32},{32,0},{64,96},{96,64},{1,33},{33,1},{65,97},{97,65},{2,34}... | collective-permute-start | bytes 3145736 | tf_op jit(solution)/shard_map/ppermute | solution.py:416
  5.3 4.7 %collective-permute-start.5 = (f32[8,256,128]{2,1,0:T(8,128)S(1)}, f32[8,256,128]{2,1,0:T(8,128)S(1)}, u32[]{:S(2)}, u32[]{:S(2)}) collective-permute-start(f32[8,256,128]{2,1,0:T(8,128)S(1)} %get-tuple-element.55), channel_id=1, source_target_pairs={{32,64},{64,32},{33,65},{65,33},{34,66},{66,34},{35,67},{67,35},{3... | collective-permute-start | bytes 3145736 | tf_op jit(solution)/shard_map/ppermute | solution.py:416
  9.9 3.9 %collective-permute-start = (f32[256,128]{1,0:T(8,128)S(1)}, f32[256,128]{1,0:T(8,128)S(1)}, u32[]{:S(2)}, u32[]{:S(2)}) collective-permute-start(f32[256,128]{1,0:T(8,128)S(1)} %get-tuple-element.37), channel_id=1, source_target_pairs={{0,7},{1,0},{2,1},{3,2},{4,3},{5,4},{6,5},{7,6},{8,15},{9,8},{10,9... | collective-permute-start | bytes 393224 | tf_op jit(solution)/shard_map/ppermute | solution.py:416
  13.8 0.0 collective-permute-start.1
  13.8 12.1 %collective-permute-done.zr = f32[256,128]{1,0:T(8,128)S(1)} collective-permute-done((f32[256,128]{1,0:T(8,128)S(1)}, f32[256,128]{1,0:T(8,128)S(1)}, u32[]{:S(2)}, u32[]{:S(2)}) %collective-permute-start) | collective-permute-done | bytes 131104 | tf_op jit(solution)/shard_map/ppermute | solution.py:416
  25.9 4.2 %collective-permute-done.1.zl = f32[256,128]{1,0:T(8,128)S(1)} collective-permute-done((f32[256,128]{1,0:T(8,128)S(1)}, f32[256,128]{1,0:T(8,128)S(1)}, u32[]{:S(2)}, u32[]{:S(2)}) %collective-permute-start.1) | collective-permute-done | bytes 131104 | tf_op jit(solution)/shard_map/ppermute | solution.py:416
  30.1 2.8 %collective-permute-start.2 = (f32[26,8,128]{2,1,0:T(8,128)S(1)}, f32[26,8,128]{2,1,0:T(8,128)S(1)}, u32[]{:S(2)}, u32[]{:S(2)}) collective-permute-start(f32[26,8,128]{2,1,0:T(8,128)S(1)} %get-tuple-element.39), channel_id=1, source_target_pairs={{0,24},{8,0},{16,8},{24,16},{1,25},{9,1},{17,9},{25,17},{2,26},{10... | collective-permute-start | bytes 319496 | tf_op jit(solution)/shard_map/ppermute | solution.py:416
  32.9 0.0 collective-permute-start.3
  32.9 0.8 %shard_map.31 = (f32[4,288,128]{2,1,0:T(8,128)S(1)}, f32[4,288,128]{2,1,0:T(8,128)S(1)}, f32[4,288,128]{2,1,0:T(8,128)S(1)}) custom-call(f32[256,128]{1,0:T(8,128)S(1)} %collective-permute-done.zr, f32[256,128]{1,0:T(8,128)S(1)} %collective-permute-done.1.zl), custom_call_target="tpu_custom_call" | custom-call | tf_op jit(solution)/shard_map/pallas_call | solution.py:410
  33.7 0.9 %collective-permute-done.2.yr = f32[26,8,128]{2,1,0:T(8,128)S(1)} collective-permute-done((f32[26,8,128]{2,1,0:T(8,128)S(1)}, f32[26,8,128]{2,1,0:T(8,128)S(1)}, u32[]{:S(2)}, u32[]{:S(2)}) %collective-permute-start.2) | collective-permute-done | bytes 106528 | tf_op jit(solution)/shard_map/ppermute | solution.py:416
  34.6 3.0 %collective-permute-done.3.yl = f32[26,8,128]{2,1,0:T(8,128)S(1)} collective-permute-done((f32[26,8,128]{2,1,0:T(8,128)S(1)}, f32[26,8,128]{2,1,0:T(8,128)S(1)}, u32[]{:S(2)}, u32[]{:S(2)}) %collective-permute-start.3) | collective-permute-done | bytes 106528 | tf_op jit(solution)/shard_map/ppermute | solution.py:416
  37.7 0.4 shard_map.32
  38.1 0.1 collective-permute-start.6
  38.2 6.5 %collective-permute-start.7 = (f32[50,8,128]{2,1,0:T(8,128)S(1)}, f32[50,8,128]{2,1,0:T(8,128)S(1)}, u32[]{:S(2)}, u32[]{:S(2)}) collective-permute-start(f32[50,8,128]{2,1,0:T(8,128)S(1)} %get-tuple-element.57), channel_id=1, source_target_pairs={{32,64},{64,32},{33,65},{65,33},{34,66},{66,34},{35,67},{67,35},{3... | collective-permute-start | bytes 614408 | tf_op jit(solution)/shard_map/ppermute | solution.py:416
  44.7 3.9 %shard_map.33 = (f32[8,288,128]{2,1,0:T(8,128)S(1)}, f32[8,288,128]{2,1,0:T(8,128)S(1)}, f32[4,288,128]{2,1,0:T(8,128)S(1)}, f32[4,288,128]{2,1,0:T(8,128)S(1)}) custom-call(s32[1]{0:T(128)} %bitcast.flip_ref, f32[8,288,128]{2,1,0:T(8,128)S(1)} %get-tuple-element.44.bm_in, ...), custom_call_target="tpu_custom_call", output_to_operand_aliasing={{0}: (1, {}), {2}: (4, {})} | custom-call | tf_op jit(solution)/shard_map/pallas_call | solution.py:410
  48.6 0.0 collective-permute-done.6.chigh
  48.6 0.0 collective-permute-done.7.clow
  48.6 0.0 collective-permute-done.4.high
  48.7 0.0 collective-permute-done.5.low
  48.7 7.7 %shard_map.34 = (f32[8,2,256,128]{3,2,1,0:T(8,128)}, f32[8,288,128]{2,1,0:T(8,128)S(1)}, f32[8,288,128]{2,1,0:T(8,128)S(1)}, f32[4,288,128]{2,1,0:T(8,128)S(1)}, f32[4,288,128]{2,1,0:T(8,128)S(1)}) custom-call(s32[1]{0:T(128)} %bitcast.flip_ref, ...), custom_call_target="tpu_custom_call", output_to_operand_aliasing={{1}: (1, {}), {2}: (2, {}), {3}: (5, {}), {4}: (6, {})} | custom-call | tf_op jit(solution)/shard_map/pallas_call | solution.py:410
  (1 shorter events, 0.0 us)
Async XLA Ops:
  3.8 44.8 %collective-permute-start.4 = (f32[8,256,128]{2,1,0:T(8,128)S(1)}, f32[8,256,128]{2,1,0:T(8,128)S(1)}, u32[]{:S(2)}, u32[]{:S(2)}) collective-permute-start(f32[8,256,128]{2,1,0:T(8,128)S(1)} %get-tuple-element.54), channel_id=1, source_target_pairs={{0,32},{32,0},{64,96},{96,64},{1,33},{33,1},{65,97},{97,65},{2,34}... | collective-permute-start | bytes 3145736 | tf_op jit(solution)/shard_map/ppermute | solution.py:416
  5.3 43.4 %collective-permute-start.5 = (f32[8,256,128]{2,1,0:T(8,128)S(1)}, f32[8,256,128]{2,1,0:T(8,128)S(1)}, u32[]{:S(2)}, u32[]{:S(2)}) collective-permute-start(f32[8,256,128]{2,1,0:T(8,128)S(1)} %get-tuple-element.55), channel_id=1, source_target_pairs={{32,64},{64,32},{33,65},{65,33},{34,66},{66,34},{35,67},{67,35},{3... | collective-permute-start | bytes 3145736 | tf_op jit(solution)/shard_map/ppermute | solution.py:416
  9.9 15.9 %collective-permute-start = (f32[256,128]{1,0:T(8,128)S(1)}, f32[256,128]{1,0:T(8,128)S(1)}, u32[]{:S(2)}, u32[]{:S(2)}) collective-permute-start(f32[256,128]{1,0:T(8,128)S(1)} %get-tuple-element.37), channel_id=1, source_target_pairs={{0,7},{1,0},{2,1},{3,2},{4,3},{5,4},{6,5},{7,6},{8,15},{9,8},{10,9... | collective-permute-start | bytes 393224 | tf_op jit(solution)/shard_map/ppermute | solution.py:416
  13.8 16.3 %collective-permute-start.1 = (f32[256,128]{1,0:T(8,128)S(1)}, f32[256,128]{1,0:T(8,128)S(1)}, u32[]{:S(2)}, u32[]{:S(2)}) collective-permute-start(f32[256,128]{1,0:T(8,128)S(1)} %get-tuple-element.38), channel_id=1, source_target_pairs={{0,1},{1,2},{2,3},{3,4},{4,5},{5,6},{6,7},{7,0},{8,9},{9,10},{10,1... | collective-permute-start | bytes 393224 | tf_op jit(solution)/shard_map/ppermute | solution.py:416
  30.1 4.5 %collective-permute-start.2 = (f32[26,8,128]{2,1,0:T(8,128)S(1)}, f32[26,8,128]{2,1,0:T(8,128)S(1)}, u32[]{:S(2)}, u32[]{:S(2)}) collective-permute-start(f32[26,8,128]{2,1,0:T(8,128)S(1)} %get-tuple-element.39), channel_id=1, source_target_pairs={{0,24},{8,0},{16,8},{24,16},{1,25},{9,1},{17,9},{25,17},{2,26},{10... | collective-permute-start | bytes 319496 | tf_op jit(solution)/shard_map/ppermute | solution.py:416
  32.9 4.8 %collective-permute-start.3 = (f32[26,8,128]{2,1,0:T(8,128)S(1)}, f32[26,8,128]{2,1,0:T(8,128)S(1)}, u32[]{:S(2)}, u32[]{:S(2)}) collective-permute-start(f32[26,8,128]{2,1,0:T(8,128)S(1)} %get-tuple-element.40), channel_id=1, source_target_pairs={{0,8},{8,16},{16,24},{24,0},{1,9},{9,17},{17,25},{25,1},{2,10},{10... | collective-permute-start | bytes 319496 | tf_op jit(solution)/shard_map/ppermute | solution.py:416
  38.1 10.5 %collective-permute-start.6 = (f32[50,8,128]{2,1,0:T(8,128)S(1)}, f32[50,8,128]{2,1,0:T(8,128)S(1)}, u32[]{:S(2)}, u32[]{:S(2)}) collective-permute-start(f32[50,8,128]{2,1,0:T(8,128)S(1)} %get-tuple-element.56), channel_id=1, source_target_pairs={{0,32},{32,0},{64,96},{96,64},{1,33},{33,1},{65,97},{97,65},{2,34}... | collective-permute-start | bytes 614408 | tf_op jit(solution)/shard_map/ppermute | solution.py:416
  38.2 10.5 %collective-permute-start.7 = (f32[50,8,128]{2,1,0:T(8,128)S(1)}, f32[50,8,128]{2,1,0:T(8,128)S(1)}, u32[]{:S(2)}, u32[]{:S(2)}) collective-permute-start(f32[50,8,128]{2,1,0:T(8,128)S(1)} %get-tuple-element.57), channel_id=1, source_target_pairs={{32,64},{64,32},{33,65},{65,33},{34,66},{66,34},{35,67},{67,35},{3... | collective-permute-start | bytes 614408 | tf_op jit(solution)/shard_map/ppermute | solution.py:416

commit v3 on v2

--- a/solution.py
+++ b/solution.py
@@ -74,20 +74,17 @@
 
     def tile(t):
         rows = pl.ds(pl.multiple_of(t * 8, 8), 8)
-        acc = [jnp.zeros((8, 128), F32)] * 4
+        acc = [jnp.zeros((8, 128), F32)] * 3
         for q in range(Q):
             b, sr, sb = split_colours(fbuf, sbuf, mirrored(q, flip), rows, odd)
             place = 16 * segment(q)
             here = lane // 16 == segment(q)
-            parts = (
-                turn(b, place),
-                turn(jnp.where(left_half, sr, b), place + 6),
-                turn(jnp.where(left_half, sb, sr), place + 11),
-                turn(sb, place + 15),
-            )
-            acc = [jnp.where(here, new, old) for new, old in zip(parts, acc)]
+            near_here = (lane + 4) % 128 // 16 == segment(q)
+            acc[0] = jnp.where(near_here, turn(jnp.where(left_half, b, sb), place), acc[0])
+            acc[1] = jnp.where(here, turn(jnp.where(left_half, sr, b), place + 6), acc[1])
+            acc[2] = jnp.where(here, turn(jnp.where(left_half, sb, sr), place + 11), acc[2])
         zlow[rows, :] = jnp.where(col < 6, acc[0], jnp.where(col < 11, acc[1], acc[2]))
-        zhigh[rows, :] = jnp.where(col < 6, acc[1], jnp.where(col < 11, acc[2], acc[3]))
+        zhigh[rows, :] = jnp.where(col < 6, acc[1], jnp.where(col < 12, acc[2], acc[0]))
 
     for c in range(CHUNKS):
         copies[2 * c].wait()
@@ -133,48 +130,54 @@
 def put_rim(rows, r, l, place, refs):
     lane = lanes_of()
     col, half = lane % 16, lane % 64
-    one = jnp.where(col < 6, l, r)
-    two = jnp.where(col < 11, l, r)
-    parts = [turn(r, -place), turn(one, -place - 6), turn(two, -place - 11), turn(l, -place - 15)]
+    parts = [
+        turn(jnp.where(col < 12, r, l), -place),
+        turn(jnp.where(col < 6, l, r), -place - 6),
+        turn(jnp.where(col < 11, l, r), -place - 11),
+    ]
     for n, (ref, width) in enumerate(zip(refs, (6, 5, 4))):
-        ref[rows, :] = jnp.where(half < width, parts[n], jnp.where(half >= 64 - width, parts[n + 1], 0.0))
-
-
-def rim_kernel(zr, zl, bh, srh, sbh):
+        ref[rows, :] = jnp.where(half < width, parts[n], jnp.where(half >= 64 - width, parts[(n + 1) % 3], 0.0))
+
+
+def edges_low(r, l):
+    return jnp.where(lanes_of() < 60, r, turn(l, 64))
+
+
+def edges_high(r, l):
+    return jnp.where(lanes_of() < 60, turn(r, 64), l)
+
+
+def put_halo_rims(rows, low, high, refs):
+    lane = lanes_of()
+    high = turn(high, 64)
+    r = jnp.where(lane < 60, low, high)
+    l = turn(jnp.where((lane >= 60) & (lane < 124), low, high), 64)
+    for d in range(3):
+        put_rim(rows, r, l, 16 * d, [ref.at[d] for ref in refs[:3 if d < 2 else 2]])
+
+
+def edge_kernel(after, zr, zl, high, low):
+    del after
+
     def body(first, tiles):
         for u in range(tiles):
-            r = pl.multiple_of((first + u) * 8, 8)
-            for a in range(4):
-                refs = [ref.at[a] for ref in (bh, srh, sbh)]
-                put_rim(pl.ds(pl.multiple_of(r + 16, 8), 8), zr[pl.ds(r, 8), :], zl[pl.ds(r, 8), :], 16 * a, refs)
-
-    batched(TILES, 8, body)
-
-
-def corner_kernel(yr, yl, zr, zl, bm_in, srm_in, sbm_in, bh_in, srh_in, sbh_in, high, low, bm, srm, sbm, bh, srh, sbh):
+            rows = pl.ds(pl.multiple_of((first + u) * 8, 8), 8)
+            low[rows, :] = edges_low(zr[rows, :], zl[rows, :])
+            high[rows, :] = edges_high(zr[rows, :], zl[rows, :])
+
+    batched(TILES, 16, body)
+
+
+def corner_kernel(yr, yl, bm_in, srm_in, sbm_in, bh_in, srh_in, sbh_in, high, low, bm, srm, sbm, bh, srh, sbh):
     del bm_in, srm_in, sbm_in, bh_in, srh_in, sbh_in
-    lane = lanes_of()
-    left_half = lane < 64
-    for out, planes in ((low, (0, 1, 2)), (high, (7, 6, 5))):
+    for out, planes, pack in ((low, (0, 1, 2), edges_low), (high, (7, 6, 5), edges_high)):
         for side, ref in enumerate((yr, yl)):
             for d, q in enumerate(planes):
                 out[8 * side + d] = ref[q]
                 out[8 * side + 3 + d] = ref[8 + q]
                 if d < 2:
                     out[8 * side + 6 + d] = ref[16 + q]
-
-    def put(n, r, l):
-        low[n] = jnp.where(left_half, r, turn(l, 64))
-        high[n] = jnp.where(left_half, turn(r, 64), l)
-
-    def body(first, tiles):
-        for u in range(tiles):
-            rows = pl.ds(pl.multiple_of((first + u) * 8, 8), 8)
-            put(first + u + 17, zr[rows, :], zl[rows, :])
-
-    put(16, yl[24], yl[25])
-    put(49, yr[24], yr[25])
-    batched(TILES, 16, body)
+            out[16 + side] = pack(ref[24], ref[25])
     for row, ref in ((8, yl), (NY + 16, yr)):
         for q in range(Q):
             bm[q, row:row + 8, :] = ref[q]
@@ -254,7 +257,10 @@
     return done
 
 
-def sweep_rows(red, jobs, marks, main, rim, wall):
+EVERY = ((0, TILES + 2),)
+
+
+def sweep_rows(red, jobs, marks, main, rim, wall, spans=EVERY):
     dst = "red" if red else "black"
 
     def body(first, tiles):
@@ -267,70 +273,100 @@
                 for ref, value in zip((main(dst, a), main(dst, Q - 1 - a), rim(dst, a)), new):
                     ref[pl.ds(r, 8), :] = value
 
-    batched(TILES + 2, max(1, BATCH // len(jobs)), body)
+    for start, count in spans:
+        batched(count, max(1, BATCH // len(jobs)), lambda first, tiles: body(start + first, tiles))
 
 
 def full(*planes):
     return [(a, "both", None) for a in planes]
 
 
-def inner_kernel(flip_ref, bm_in, srm, sbm, bh_in, srh, sbh, bm, rm, bh, rh):
-    del bm_in, bh_in
-    marks = Marks(flip_ref[0] % 2)
-    mains = {"black": bm, "red": rm, "sr": srm, "sb": sbm}
-    edges = {"black": bh, "red": rh, "sr": srh, "sb": sbh}
-
+INNER = (
+    (True, [(0, "up", None)] + full(1, 2, 3)),
+    (False, full(1, 2, 3)),
+    (True, [(1, "up", 0)] + full(2, 3)),
+    (False, full(2, 3)),
+    (True, [(2, "up", 0)] + full(3)),
+    (False, full(3)),
+)
+EARLY = 2
+
+
+def lookups(mains, edges):
     def main(kind, q):
         return mains[kind].at[q]
 
     def rim(kind, a):
         return edges[kind].at[a]
 
-    for red, jobs in (
-        (True, [(0, "up", None)] + full(1, 2, 3)),
-        (False, full(1, 2, 3)),
-        (True, [(1, "up", 0)] + full(2, 3)),
-        (False, full(2, 3)),
-        (True, [(2, "up", 0)] + full(3)),
-        (False, full(3)),
-    ):
-        sweep_rows(red, jobs, marks, main, rim, None)
+    return main, rim
+
+
+def early_kernel(flip_ref, after, zr, zl, bm_in, srm, sbm, bm, rm, bh, rh, srh, sbh):
+    del after, bm_in
+    marks = Marks(flip_ref[0] % 2)
+
+    def body(first, tiles):
+        for u in range(tiles):
+            r = pl.multiple_of((first + u) * 8, 8)
+            for a in range(4):
+                refs = [ref.at[a] for ref in (bh, srh, sbh)]
+                put_rim(pl.ds(pl.multiple_of(r + 16, 8), 8), zr[pl.ds(r, 8), :], zl[pl.ds(r, 8), :], 16 * a, refs)
+
+    batched(TILES, 8, body)
+    main, rim = lookups({"black": bm, "red": rm, "sr": srm, "sb": sbm}, {"black": bh, "red": rh, "sr": srh, "sb": sbh})
+    for n, (red, jobs) in enumerate(INNER[:EARLY]):
+        sweep_rows(red, jobs, marks, main, rim, None, ((2 + n, TILES - 2 - 2 * n),))
+
+
+def inner_kernel(flip_ref, bm_in, rm_in, srm, sbm, bh_in, rh_in, srh, sbh, bm, rm, bh, rh):
+    del bm_in, rm_in, bh_in, rh_in
+    marks = Marks(flip_ref[0] % 2)
+    main, rim = lookups({"black": bm, "red": rm, "sr": srm, "sb": sbm}, {"black": bh, "red": rh, "sr": srh, "sb": sbh})
+    for n, (red, jobs) in enumerate(INNER):
+        spans = ((0, 2 + n), (TILES - n, 2 + n)) if n < EARLY else EVERY
+        sweep_rows(red, jobs, marks, main, rim, None, spans)
+
+
+def halo_kernel(after, high, low, ehigh, elow, xbm, xsrm, xsbm, xbh, xsrh, xsbh):
+    del after
+
+    def body(first, tiles):
+        for u in range(tiles):
+            r = pl.multiple_of((first + u) * 8, 8)
+            rows, put = pl.ds(r, 8), pl.ds(pl.multiple_of(r + 16, 8), 8)
+            for side, face in enumerate((low, high)):
+                for d in range(3):
+                    xbm[3 * side + d, put, :] = face[d, rows, :]
+                    xsrm[3 * side + d, put, :] = face[3 + d, rows, :]
+                    if d < 2:
+                        xsbm[2 * side + d, put, :] = face[6 + d, rows, :]
+            put_halo_rims(put, elow[rows, :], ehigh[rows, :], (xbh, xsrh, xsbh))
+
+    batched(TILES, 8, body)
 
 
 OUT_CHUNKS = 4
 
 
-def outer_kernel(flip_ref, bm_in, rm_in, srm, sbm, bh_in, rh_in, srh, sbh, high, low, chigh, clow,
-                 out, bm, rm, bh, rh, xbm, xbh, xrm, xrh, xsrm, xsrh, xsbm, xsbh, obuf, sems):
-    del bm_in, rm_in, bh_in, rh_in
+def outer_kernel(flip_ref, bm_in, rm_in, srm, sbm, bh_in, rh_in, srh, sbh, chigh, clow,
+                 xbm_in, xsrm_in, xsbm_in, xbh_in, xsrh_in, xsbh_in,
+                 out, bm, rm, bh, rh, xbm, xsrm, xsbm, xbh, xsrh, xsbh, xrm, xrh, obuf, sems):
+    del bm_in, rm_in, bh_in, rh_in, xbm_in, xsrm_in, xsbm_in, xbh_in, xsrh_in, xsbh_in
     flip = flip_ref[0] % 2
     marks = Marks(flip)
-    lane = marks.lane
     outside = jnp.where(flip_ref[0] >= 2, 0.0, SIXTH)
     wall = (outside, SIXTH, jnp.where(marks.turned, SIXTH, outside))
     plain = odd_cells() == 1
 
-    for side, face, corner in ((0, low, clow), (1, high, chigh)):
-        for d in range(3):
-            for n, (ref, deep) in enumerate(((xbm, 3), (xsrm, 3), (xsbm, 2))):
-                if d < deep:
-                    slot = deep * side + d
-                    ref[slot, 8:16, :] = corner[8 + 3 * n + d]
-                    ref[slot, 16:NY + 16, :] = face[3 * n + d]
-                    ref[slot, NY + 16:NY + 24, :] = corner[3 * n + d]
-
-    def fill(first, tiles):
-        for u in range(tiles):
-            t = first + u
-            rows = pl.ds(pl.multiple_of(t * 8 + 8, 8), 8)
-            one = clow[16 + t]
-            two = turn(chigh[16 + t], 64)
-            r = jnp.where(lane < 64, one, two)
-            l = turn(jnp.where(lane < 64, two, one), 64)
+    for y, (row, n) in enumerate(((NY + 16, 0), (8, 8))):
+        for side, corner in enumerate((clow, chigh)):
             for d in range(3):
-                put_rim(rows, r, l, 16 * d, [ref.at[d] for ref in (xbh, xsrh, xsbh)[:3 if d < 2 else 2]])
-
-    batched(TILES + 2, 8, fill)
+                xbm[3 * side + d, row:row + 8, :] = corner[n + d]
+                xsrm[3 * side + d, row:row + 8, :] = corner[n + 3 + d]
+                if d < 2:
+                    xsbm[2 * side + d, row:row + 8, :] = corner[n + 6 + d]
+        put_halo_rims(pl.ds(row, 8), clow[16 + y], chigh[16 + y], (xbh, xsrh, xsbh))
 
     mains = {"black": (bm, xbm), "red": (rm, xrm), "sr": (srm, xsrm), "sb": (sbm, xsbm)}
     edges = {"black": (bh, xbh), "red": (rh, xrh), "sr": (srh, xsrh), "sb": (sbh, xsbh)}
@@ -431,7 +467,7 @@
     ]
     edge = VM((4, ROWS, NZ), F32)
     work, face, block = VM((Q, ROWS, NZ), F32), VM((Q, NY, NZ), F32), VM((Q, 2, NY, NZ), F32)
-    rows, strip, corner = VM((NY, NZ), F32), VM((26, 8, NZ), F32), VM((50, 8, NZ), F32)
+    rows, strip, corner = VM((NY, NZ), F32), VM((26, 8, NZ), F32), VM((18, 8, NZ), F32)
 
     fbuf, sbuf, zlow, zhigh = kernel(
         pack_kernel, 2, (block, block, rows, rows), [flip] + blocks,
@@ -445,23 +481,33 @@
     ylow, yhigh = kernel(y_kernel, 2, (strip, strip), [bm, srm, sbm, zr, zl])
     yr = send(ylow, "gy", ring(ny, -1))
     yl = send(yhigh, "gy", ring(ny, 1))
-    bh, srh, sbh = kernel(rim_kernel, 2, (edge,) * 3, [zr, zl])
+    ehigh, elow = kernel(edge_kernel, 2, (rows, rows), [(ylow, hbm()), zr, zl])
+    ehigh = send(ehigh, "gx", chip)
+    elow = send(elow, "gx", across)
+    bm, rm, bh, rh, srh, sbh = kernel(
+        early_kernel, 4, (work, work) + (edge,) * 4, [flip, (ylow, hbm()), zr, zl, bm, srm, sbm],
+        input_output_aliases={4: 0},
+    )
     chigh, clow, bm, srm, sbm, bh, srh, sbh = kernel(
-        corner_kernel, 2, (corner, corner) + (work,) * 3 + (edge,) * 3, [yr, yl, zr, zl, bm, srm, sbm, bh, srh, sbh],
-        input_output_aliases={4 + i: 2 + i for i in range(6)},
+        corner_kernel, 2, (corner, corner) + (work,) * 3 + (edge,) * 3, [yr, yl, bm, srm, sbm, bh, srh, sbh],
+        input_output_aliases={2 + i: 2 + i for i in range(6)},
     )
+    turn_of_halo = clow
     chigh = send(chigh, "gx", chip)
     clow = send(clow, "gx", across)
     bm, rm, bh, rh = kernel(
-        inner_kernel, 4, (work, work, edge, edge), [flip, bm, srm, sbm, bh, srh, sbh], input_output_aliases={1: 0, 4: 2}
+        inner_kernel, 4, (work, work, edge, edge), [flip, bm, rm, srm, sbm, bh, rh, srh, sbh],
+        input_output_aliases={1: 0, 2: 1, 5: 2, 6: 3},
     )
-    halo = [VM((n, ROWS, NZ), F32) for n in (6, 3, 6, 3, 6, 3, 4, 2)]
+    halo = [VM((n, ROWS, NZ), F32) for n in (6, 6, 4, 3, 3, 2)]
+    halos = kernel(halo_kernel, 2, halo, [(turn_of_halo, hbm()), high, low, ehigh, elow])
     out = kernel(
-        outer_kernel, 16, (jax.ShapeDtypeStruct((Q, 2, NY, NZ), F32), work, work, edge, edge),
-        [flip, bm, rm, srm, sbm, bh, rh, srh, sbh, high, low, chigh, clow],
-        out_specs=[hbm()] + [pl.BlockSpec(memory_space=VM)] * 4,
-        input_output_aliases={1: 1, 2: 2, 5: 3, 6: 4},
-        scratch_shapes=halo + [block, pltpu.SemaphoreType.DMA((OUT_CHUNKS,))],
+        outer_kernel, 12,
+        [jax.ShapeDtypeStruct((Q, 2, NY, NZ), F32), work, work, edge, edge] + halo,
+        [flip, bm, rm, srm, sbm, bh, rh, srh, sbh, chigh, clow, *halos],
+        out_specs=[hbm()] + [pl.BlockSpec(memory_space=VM)] * 10,
+        input_output_aliases={1: 1, 2: 2, 5: 3, 6: 4, **{11 + i: 5 + i for i in range(6)}},
+        scratch_shapes=[halo[0], halo[3], block, pltpu.SemaphoreType.DMA((OUT_CHUNKS,))],
     )[0]
     return out.reshape(field.shape)
 

time: 56.7 us -> 56.8 us (level)
  starting transfers between devices: 19.4 us -> 21.1 us
  waiting for transfers between devices: 20.3 us -> 19.4 us
  Pallas kernels: 16.6 us -> 15.8 us
    ppermute x8 -> x10, starting transfers between devices: 19.4 us -> 21.1 us  [send(): return lax.ppermute(near(value), axis, pairs)]
    ppermute x8 -> x10, waiting for transfers between devices: 20.3 us -> 19.4 us  [send(): return lax.ppermute(near(value), axis, pairs)]
    pallas_call x7 -> x9, Pallas kernels: 16.6 us -> 15.8 us  [kernel(): pl.pallas_call(body, out_shape=outs, in_specs=specs, out_specs=out_specs,...]
  transfers between devices with their start and end apart: 8 -> 10, of which waited for: 4 -> 4; matrix products, arithmetic and copies ran while one was open for 0% -> 0% of each run, Pallas kernels for 9% -> 11%
where the time goes in v3:
time: 56.8 us; the launch traced here: 56.7 us
  starting transfers between devices  21.1 us (37%)
  waiting for transfers between devices  19.4 us (34%)
  Pallas kernels  15.8 us (28%)
    ppermute x10, starting transfers between devices, send(): return lax.ppermute(near(value), axis, pairs)  21.1 us
    ppermute x10, waiting for transfers between devices, send(): return lax.ppermute(near(value), axis, pairs)  19.4 us
    pallas_call x9, Pallas kernels, kernel(): pl.pallas_call(body, out_shape=outs, in_specs=specs, out_specs=out_specs,...  15.8 us
  transfers between devices with their start and end apart: 10, of which 4 were waited for; matrix products, arithmetic and copies ran while one was open for 0% of the time, Pallas kernels for 11%

profile of v3, /device:TPU:1, one launch (start us, length us, event | category | flops | bytes accessed | tf_op | source)
XLA Modules:
  0.0 56.7 jit_solution(18443172720040617304)
XLA Ops:
  0.0 2.5 %shard_map.28 = (f32[8,2,256,128]{3,2,1,0:T(8,128)S(1)}, f32[8,2,256,128]{3,2,1,0:T(8,128)S(1)}, f32[256,128]{1,0:T(8,128)S(1)}, f32[256,128]{1,0:T(8,128)S(1)}) custom-call(s32[1]{0:T(128)} %bitcast.flip_ref, f32[8,2,256,128]{3,2,1,0:T(8,128)} %bitcast.4, f32[8,2,256,128]{3,2,1,0:T(8,128)} %bitcast.5), custom_call_target="tpu_custom_call" | custom-call | tf_op jit(solution)/shard_map/pallas_call | solution.py:446
  2.6 1.0 %shard_map.29 = (f32[8,288,128]{2,1,0:T(8,128)S(1)}, f32[8,288,128]{2,1,0:T(8,128)S(1)}, f32[8,288,128]{2,1,0:T(8,128)S(1)}, f32[8,256,128]{2,1,0:T(8,128)S(1)}, f32[8,256,128]{2,1,0:T(8,128)S(1)}) custom-call(s32[1]{0:T(128)} %bitcast.flip_ref, f32[8,2,256,128]{3,2,1,0:T(8,128)S(1)} %get-tuple-element.43.fbuf, f32[8,2,256,128]{3,2,1,0:T(8,128)S(1)} %get-tuple-element.44.sbuf), custom_call_target="tpu_custom_call" | custom-call | tf_op jit(solution)/shard_map/pallas_call | solution.py:446
  3.6 1.5 %collective-permute-start.6 = (f32[8,256,128]{2,1,0:T(8,128)S(1)}, f32[8,256,128]{2,1,0:T(8,128)S(1)}, u32[]{:S(2)}, u32[]{:S(2)}) collective-permute-start(f32[8,256,128]{2,1,0:T(8,128)S(1)} %get-tuple-element.70), channel_id=1, source_target_pairs={{0,32},{32,0},{64,96},{96,64},{1,33},{33,1},{65,97},{97,65},{2,34}... | collective-permute-start | bytes 3145736 | tf_op jit(solution)/shard_map/ppermute | solution.py:452
  5.0 4.7 %collective-permute-start.7 = (f32[8,256,128]{2,1,0:T(8,128)S(1)}, f32[8,256,128]{2,1,0:T(8,128)S(1)}, u32[]{:S(2)}, u32[]{:S(2)}) collective-permute-start(f32[8,256,128]{2,1,0:T(8,128)S(1)} %get-tuple-element.71), channel_id=1, source_target_pairs={{32,64},{64,32},{33,65},{65,33},{34,66},{66,34},{35,67},{67,35},{3... | collective-permute-start | bytes 3145736 | tf_op jit(solution)/shard_map/ppermute | solution.py:452
  9.7 3.9 %collective-permute-start = (f32[256,128]{1,0:T(8,128)S(1)}, f32[256,128]{1,0:T(8,128)S(1)}, u32[]{:S(2)}, u32[]{:S(2)}) collective-permute-start(f32[256,128]{1,0:T(8,128)S(1)} %get-tuple-element.48), channel_id=1, source_target_pairs={{0,7},{1,0},{2,1},{3,2},{4,3},{5,4},{6,5},{7,6},{8,15},{9,8},{10,9... | collective-permute-start | bytes 393224 | tf_op jit(solution)/shard_map/ppermute | solution.py:452
  13.6 0.0 collective-permute-start.1
  13.6 12.1 %collective-permute-done.zr = f32[256,128]{1,0:T(8,128)S(1)} collective-permute-done((f32[256,128]{1,0:T(8,128)S(1)}, f32[256,128]{1,0:T(8,128)S(1)}, u32[]{:S(2)}, u32[]{:S(2)}) %collective-permute-start) | collective-permute-done | bytes 131104 | tf_op jit(solution)/shard_map/ppermute | solution.py:452
  25.6 4.2 %collective-permute-done.1.zl = f32[256,128]{1,0:T(8,128)S(1)} collective-permute-done((f32[256,128]{1,0:T(8,128)S(1)}, f32[256,128]{1,0:T(8,128)S(1)}, u32[]{:S(2)}, u32[]{:S(2)}) %collective-permute-start.1) | collective-permute-done | bytes 131104 | tf_op jit(solution)/shard_map/ppermute | solution.py:452
  29.9 1.4 %collective-permute-start.3 = (f32[26,8,128]{2,1,0:T(8,128)S(1)}, f32[26,8,128]{2,1,0:T(8,128)S(1)}, u32[]{:S(2)}, u32[]{:S(2)}) collective-permute-start(f32[26,8,128]{2,1,0:T(8,128)S(1)} %get-tuple-element.51), channel_id=1, source_target_pairs={{0,8},{8,16},{16,24},{24,0},{1,9},{9,17},{17,25},{25,1},{2,10},{10... | collective-permute-start | bytes 319496 | tf_op jit(solution)/shard_map/ppermute | solution.py:452
  31.2 0.2 shard_map.34
  31.4 0.1 collective-permute-start.8
  31.5 1.5 %collective-permute-start.2 = (f32[26,8,128]{2,1,0:T(8,128)S(1)}, f32[26,8,128]{2,1,0:T(8,128)S(1)}, u32[]{:S(2)}, u32[]{:S(2)}) collective-permute-start(f32[26,8,128]{2,1,0:T(8,128)S(1)} %get-tuple-element.50.after), channel_id=1, source_target_pairs={{0,24},{8,0},{16,8},{24,16},{1,25},{9,1},{17,9},{25,17},{2,26},{10... | collective-permute-start | bytes 319496 | tf_op jit(solution)/shard_map/ppermute | solution.py:452
  33.1 1.7 %collective-permute-done.3.yl = f32[26,8,128]{2,1,0:T(8,128)S(1)} collective-permute-done((f32[26,8,128]{2,1,0:T(8,128)S(1)}, f32[26,8,128]{2,1,0:T(8,128)S(1)}, u32[]{:S(2)}, u32[]{:S(2)}) %collective-permute-start.3) | collective-permute-done | bytes 106528 | tf_op jit(solution)/shard_map/ppermute | solution.py:452
  34.8 6.0 %collective-permute-start.9 = (f32[256,128]{1,0:T(8,128)S(1)}, f32[256,128]{1,0:T(8,128)S(1)}, u32[]{:S(2)}, u32[]{:S(2)}) collective-permute-start(f32[256,128]{1,0:T(8,128)S(1)} %get-tuple-element.73), channel_id=1, source_target_pairs={{32,64},{64,32},{33,65},{65,33},{34,66},{66,34},{35,67},{67,35},{3... | collective-permute-start | bytes 393224 | tf_op jit(solution)/shard_map/ppermute | solution.py:452
  40.7 2.2 %shard_map.31 = (f32[8,288,128]{2,1,0:T(8,128)S(1)}, f32[8,288,128]{2,1,0:T(8,128)S(1)}, f32[4,288,128]{2,1,0:T(8,128)S(1)}, f32[4,288,128]{2,1,0:T(8,128)S(1)},...) custom-call(s32[1]{0:T(128)} %bitcast.flip_ref, ...), custom_call_target="tpu_custom_call", output_to_operand_aliasing={{0}: (4, {})} | custom-call | tf_op jit(solution)/shard_map/pallas_call | solution.py:446
  43.0 0.0 collective-permute-done.2.yr
  43.0 0.1 shard_map.32
  43.1 0.1 collective-permute-start.4
  43.2 0.0 collective-permute-done.8.ehigh
  43.2 2.1 %collective-permute-start.5 = (f32[18,8,128]{2,1,0:T(8,128)S(1)}, f32[18,8,128]{2,1,0:T(8,128)S(1)}, u32[]{:S(2)}, u32[]{:S(2)}) collective-permute-start(f32[18,8,128]{2,1,0:T(8,128)S(1)} %get-tuple-element.69.after), channel_id=1, source_target_pairs={{32,64},{64,32},{33,65},{65,33},{34,66},{66,34},{35,67},{67,35},{3... | collective-permute-start | bytes 221192 | tf_op jit(solution)/shard_map/ppermute | solution.py:452
  45.3 2.5 %shard_map.33 = (f32[8,288,128]{2,1,0:T(8,128)S(1)}, f32[8,288,128]{2,1,0:T(8,128)S(1)}, f32[4,288,128]{2,1,0:T(8,128)S(1)}, f32[4,288,128]{2,1,0:T(8,128)S(1)}) custom-call(s32[1]{0:T(128)} %bitcast.flip_ref, f32[8,288,128]{2,1,0:T(8,128)S(1)} %get-tuple-element.56.bm_in, ...), custom_call_target="tpu_custom_call", output_to_operand_aliasing={{0}: (1, {}), {1}: (2, {}), {2}: (5, {}), {3}: (6, {})} | custom-call | tf_op jit(solution)/shard_map/pallas_call | solution.py:446
  47.8 0.0 collective-permute-done.9.elow
  47.8 0.0 collective-permute-done.6.high
  47.8 0.0 collective-permute-done.7.low
  47.8 1.1 %shard_map.35 = (f32[6,288,128]{2,1,0:T(8,128)S(1)}, f32[6,288,128]{2,1,0:T(8,128)S(1)}, f32[4,288,128]{2,1,0:T(8,128)S(1)}, f32[3,288,128]{2,1,0:T(8,128)S(1)},...) custom-call(f32[18,8,128]{2,1,0:T(8,128)S(1)} %get-tuple-element.69.after, ...), custom_call_target="tpu_custom_call" | custom-call | tf_op jit(solution)/shard_map/pallas_call | solution.py:446
  48.9 0.0 collective-permute-done.4.chigh
  48.9 1.4 %collective-permute-done.5.clow = f32[18,8,128]{2,1,0:T(8,128)S(1)} collective-permute-done((f32[18,8,128]{2,1,0:T(8,128)S(1)}, f32[18,8,128]{2,1,0:T(8,128)S(1)}, u32[]{:S(2)}, u32[]{:S(2)}) %collective-permute-start.5) | collective-permute-done | bytes 73760 | tf_op jit(solution)/shard_map/ppermute | solution.py:452
  50.4 6.1 %shard_map.36 = (f32[8,2,256,128]{3,2,1,0:T(8,128)}, f32[8,288,128]{2,1,0:T(8,128)S(1)}, f32[8,288,128]{2,1,0:T(8,128)S(1)}, f32[4,288,128]{2,1,0:T(8,128)S(1)},...) custom-call(s32[1]{0:T(128)} %bitcast.flip_ref, ...), custom_call_target="tpu_custom_call", output_to_operand_aliasing={{1}: (1, {}), {2}: (2, {}), {3}: (5, {}), {4}: (6, {}), {5}... | custom-call | tf_op jit(solution)/shard_map/pallas_call | solution.py:446
  (1 shorter events, 0.0 us)
Async XLA Ops:
  3.6 44.2 %collective-permute-start.6 = (f32[8,256,128]{2,1,0:T(8,128)S(1)}, f32[8,256,128]{2,1,0:T(8,128)S(1)}, u32[]{:S(2)}, u32[]{:S(2)}) collective-permute-start(f32[8,256,128]{2,1,0:T(8,128)S(1)} %get-tuple-element.70), channel_id=1, source_target_pairs={{0,32},{32,0},{64,96},{96,64},{1,33},{33,1},{65,97},{97,65},{2,34}... | collective-permute-start | bytes 3145736 | tf_op jit(solution)/shard_map/ppermute | solution.py:452
  5.0 42.8 %collective-permute-start.7 = (f32[8,256,128]{2,1,0:T(8,128)S(1)}, f32[8,256,128]{2,1,0:T(8,128)S(1)}, u32[]{:S(2)}, u32[]{:S(2)}) collective-permute-start(f32[8,256,128]{2,1,0:T(8,128)S(1)} %get-tuple-element.71), channel_id=1, source_target_pairs={{32,64},{64,32},{33,65},{65,33},{34,66},{66,34},{35,67},{67,35},{3... | collective-permute-start | bytes 3145736 | tf_op jit(solution)/shard_map/ppermute | solution.py:452
  9.7 15.9 %collective-permute-start = (f32[256,128]{1,0:T(8,128)S(1)}, f32[256,128]{1,0:T(8,128)S(1)}, u32[]{:S(2)}, u32[]{:S(2)}) collective-permute-start(f32[256,128]{1,0:T(8,128)S(1)} %get-tuple-element.48), channel_id=1, source_target_pairs={{0,7},{1,0},{2,1},{3,2},{4,3},{5,4},{6,5},{7,6},{8,15},{9,8},{10,9... | collective-permute-start | bytes 393224 | tf_op jit(solution)/shard_map/ppermute | solution.py:452
  13.6 16.3 %collective-permute-start.1 = (f32[256,128]{1,0:T(8,128)S(1)}, f32[256,128]{1,0:T(8,128)S(1)}, u32[]{:S(2)}, u32[]{:S(2)}) collective-permute-start(f32[256,128]{1,0:T(8,128)S(1)} %get-tuple-element.49), channel_id=1, source_target_pairs={{0,1},{1,2},{2,3},{3,4},{4,5},{5,6},{6,7},{7,0},{8,9},{9,10},{10,1... | collective-permute-start | bytes 393224 | tf_op jit(solution)/shard_map/ppermute | solution.py:452
  29.9 4.9 %collective-permute-start.3 = (f32[26,8,128]{2,1,0:T(8,128)S(1)}, f32[26,8,128]{2,1,0:T(8,128)S(1)}, u32[]{:S(2)}, u32[]{:S(2)}) collective-permute-start(f32[26,8,128]{2,1,0:T(8,128)S(1)} %get-tuple-element.51), channel_id=1, source_target_pairs={{0,8},{8,16},{16,24},{24,0},{1,9},{9,17},{17,25},{25,1},{2,10},{10... | collective-permute-start | bytes 319496 | tf_op jit(solution)/shard_map/ppermute | solution.py:452
  31.4 11.7 %collective-permute-start.8 = (f32[256,128]{1,0:T(8,128)S(1)}, f32[256,128]{1,0:T(8,128)S(1)}, u32[]{:S(2)}, u32[]{:S(2)}) collective-permute-start(f32[256,128]{1,0:T(8,128)S(1)} %get-tuple-element.72), channel_id=1, source_target_pairs={{0,32},{32,0},{64,96},{96,64},{1,33},{33,1},{65,97},{97,65},{2,34}... | collective-permute-start | bytes 393224 | tf_op jit(solution)/shard_map/ppermute | solution.py:452
  31.5 11.4 %collective-permute-start.2 = (f32[26,8,128]{2,1,0:T(8,128)S(1)}, f32[26,8,128]{2,1,0:T(8,128)S(1)}, u32[]{:S(2)}, u32[]{:S(2)}) collective-permute-start(f32[26,8,128]{2,1,0:T(8,128)S(1)} %get-tuple-element.50.after), channel_id=1, source_target_pairs={{0,24},{8,0},{16,8},{24,16},{1,25},{9,1},{17,9},{25,17},{2,26},{10... | collective-permute-start | bytes 319496 | tf_op jit(solution)/shard_map/ppermute | solution.py:452
  34.8 13.0 %collective-permute-start.9 = (f32[256,128]{1,0:T(8,128)S(1)}, f32[256,128]{1,0:T(8,128)S(1)}, u32[]{:S(2)}, u32[]{:S(2)}) collective-permute-start(f32[256,128]{1,0:T(8,128)S(1)} %get-tuple-element.73), channel_id=1, source_target_pairs={{32,64},{64,32},{33,65},{65,33},{34,66},{66,34},{35,67},{67,35},{3... | collective-permute-start | bytes 393224 | tf_op jit(solution)/shard_map/ppermute | solution.py:452
  43.1 5.9 %collective-permute-start.4 = (f32[18,8,128]{2,1,0:T(8,128)S(1)}, f32[18,8,128]{2,1,0:T(8,128)S(1)}, u32[]{:S(2)}, u32[]{:S(2)}) collective-permute-start(f32[18,8,128]{2,1,0:T(8,128)S(1)} %get-tuple-element.68), channel_id=1, source_target_pairs={{0,32},{32,0},{64,96},{96,64},{1,33},{33,1},{65,97},{97,65},{2,34}... | collective-permute-start | bytes 221192 | tf_op jit(solution)/shard_map/ppermute | solution.py:452
  43.2 7.2 %collective-permute-start.5 = (f32[18,8,128]{2,1,0:T(8,128)S(1)}, f32[18,8,128]{2,1,0:T(8,128)S(1)}, u32[]{:S(2)}, u32[]{:S(2)}) collective-permute-start(f32[18,8,128]{2,1,0:T(8,128)S(1)} %get-tuple-element.69.after), channel_id=1, source_target_pairs={{32,64},{64,32},{33,65},{65,33},{34,66},{66,34},{35,67},{67,35},{3... | collective-permute-start | bytes 221192 | tf_op jit(solution)/shard_map/ppermute | solution.py:452

commit v4 on v3

--- a/solution.py
+++ b/solution.py
@@ -110,21 +110,42 @@
                     ref[q, put, :] = v
                 out, d = (low, q) if q < 4 else (high, Q - 1 - q)
                 if d < 3:
-                    out[d, rows, :] = values[0]
-                    out[3 + d, rows, :] = values[1]
+                    out[d, put, :] = values[0]
+                    out[3 + d, put, :] = values[1]
                 if d < 2:
-                    out[6 + d, rows, :] = values[2]
+                    out[6 + d, put, :] = values[2]
 
     batched(TILES, 4, body)
 
 
+def rows_of():
+    return lax.broadcasted_iota(jnp.int32, (8, 128), 0)
+
+
+def pack_low(b, sr, sb):
+    row = rows_of()
+    return jnp.where(row < 6, b, pltpu.roll(sr, 3, 0)), jnp.where(row < 4, sb, pltpu.roll(sr, 4, 0))
+
+
+def unpack_low(one, two):
+    return one, jnp.where(rows_of() < 3, pltpu.roll(two, 4, 0), pltpu.roll(one, 5, 0)), two
+
+
+def pack_high(b, sr, sb):
+    row = rows_of()
+    return jnp.where(row >= 2, b, pltpu.roll(sr, 5, 0)), jnp.where(row >= 4, sb, pltpu.roll(sr, 4, 0))
+
+
+def unpack_high(one, two):
+    return one, jnp.where(rows_of() >= 5, pltpu.roll(two, 4, 0), pltpu.roll(one, 3, 0)), two
+
+
 def y_kernel(bm, srm, sbm, zr, zl, ylow, yhigh):
-    for out, row in ((ylow, 0), (yhigh, NY - 8)):
-        for n, ref in enumerate((bm, srm, sbm)):
-            for q in range(Q):
-                out[8 * n + q] = ref[q, row + 16:row + 24, :]
-        out[24] = zr[row:row + 8, :]
-        out[25] = zl[row:row + 8, :]
+    for out, row, pack in ((ylow, 0, pack_low), (yhigh, NY - 8, pack_high)):
+        for q in range(Q):
+            out[q], out[8 + q] = pack(*(ref[q, row + 16:row + 24, :] for ref in (bm, srm, sbm)))
+        out[16] = zr[row:row + 8, :]
+        out[17] = zl[row:row + 8, :]
 
 
 def put_rim(rows, r, l, place, refs):
@@ -170,21 +191,20 @@
 
 def corner_kernel(yr, yl, bm_in, srm_in, sbm_in, bh_in, srh_in, sbh_in, high, low, bm, srm, sbm, bh, srh, sbh):
     del bm_in, srm_in, sbm_in, bh_in, srh_in, sbh_in
-    for out, planes, pack in ((low, (0, 1, 2), edges_low), (high, (7, 6, 5), edges_high)):
-        for side, ref in enumerate((yr, yl)):
-            for d, q in enumerate(planes):
-                out[8 * side + d] = ref[q]
-                out[8 * side + 3 + d] = ref[8 + q]
-                if d < 2:
-                    out[8 * side + 6 + d] = ref[16 + q]
-            out[16 + side] = pack(ref[24], ref[25])
-    for row, ref in ((8, yl), (NY + 16, yr)):
+    for side, (ref, row, unpack) in enumerate(((yr, NY + 16, unpack_low), (yl, 8, unpack_high))):
         for q in range(Q):
-            bm[q, row:row + 8, :] = ref[q]
-            srm[q, row:row + 8, :] = ref[8 + q]
-            sbm[q, row:row + 8, :] = ref[16 + q]
+            values = unpack(ref[q], ref[8 + q])
+            for array, v in zip((bm, srm, sbm), values):
+                array[q, row:row + 8, :] = v
+            out, d = (low, q) if q < 4 else (high, Q - 1 - q)
+            if d < 3:
+                out[8 * side + d], out[8 * side + 3 + d] = values[:2]
+            if d < 2:
+                out[8 * side + 6 + d] = values[2]
+        low[16 + side] = edges_low(ref[16], ref[17])
+        high[16 + side] = edges_high(ref[16], ref[17])
         for a in range(4):
-            put_rim(pl.ds(row, 8), ref[24], ref[25], 16 * a, [rim.at[a] for rim in (bh, srh, sbh)])
+            put_rim(pl.ds(row, 8), ref[16], ref[17], 16 * a, [rim.at[a] for rim in (bh, srh, sbh)])
 
 
 class Marks:
@@ -289,7 +309,7 @@
     (True, [(2, "up", 0)] + full(3)),
     (False, full(3)),
 )
-EARLY = 2
+EARLY = 1
 
 
 def lookups(mains, edges):
@@ -328,31 +348,28 @@
         sweep_rows(red, jobs, marks, main, rim, None, spans)
 
 
-def halo_kernel(after, high, low, ehigh, elow, xbm, xsrm, xsbm, xbh, xsrh, xsbh):
+def halo_kernel(after, ehigh, elow, xbh, xsrh, xsbh):
     del after
 
     def body(first, tiles):
         for u in range(tiles):
             r = pl.multiple_of((first + u) * 8, 8)
-            rows, put = pl.ds(r, 8), pl.ds(pl.multiple_of(r + 16, 8), 8)
-            for side, face in enumerate((low, high)):
-                for d in range(3):
-                    xbm[3 * side + d, put, :] = face[d, rows, :]
-                    xsrm[3 * side + d, put, :] = face[3 + d, rows, :]
-                    if d < 2:
-                        xsbm[2 * side + d, put, :] = face[6 + d, rows, :]
-            put_halo_rims(put, elow[rows, :], ehigh[rows, :], (xbh, xsrh, xsbh))
-
-    batched(TILES, 8, body)
+            put = pl.ds(pl.multiple_of(r + 16, 8), 8)
+            put_halo_rims(put, elow[pl.ds(r, 8), :], ehigh[pl.ds(r, 8), :], (xbh, xsrh, xsbh))
+
+    batched(TILES, 16, body)
 
 
 OUT_CHUNKS = 4
 
 
+SLOTS = {"black": 0, "sr": 3, "sb": 6}
+
+
 def outer_kernel(flip_ref, bm_in, rm_in, srm, sbm, bh_in, rh_in, srh, sbh, chigh, clow,
-                 xbm_in, xsrm_in, xsbm_in, xbh_in, xsrh_in, xsbh_in,
-                 out, bm, rm, bh, rh, xbm, xsrm, xsbm, xbh, xsrh, xsbh, xrm, xrh, obuf, sems):
-    del bm_in, rm_in, bh_in, rh_in, xbm_in, xsrm_in, xsbm_in, xbh_in, xsrh_in, xsbh_in
+                 low_in, high_in, xbh_in, xsrh_in, xsbh_in,
+                 out, bm, rm, bh, rh, low, high, xbh, xsrh, xsbh, xrm, xrh, obuf, sems):
+    del bm_in, rm_in, bh_in, rh_in, low_in, high_in, xbh_in, xsrh_in, xsbh_in
     flip = flip_ref[0] % 2
     marks = Marks(flip)
     outside = jnp.where(flip_ref[0] >= 2, 0.0, SIXTH)
@@ -360,22 +377,21 @@
     plain = odd_cells() == 1
 
     for y, (row, n) in enumerate(((NY + 16, 0), (8, 8))):
-        for side, corner in enumerate((clow, chigh)):
-            for d in range(3):
-                xbm[3 * side + d, row:row + 8, :] = corner[n + d]
-                xsrm[3 * side + d, row:row + 8, :] = corner[n + 3 + d]
-                if d < 2:
-                    xsbm[2 * side + d, row:row + 8, :] = corner[n + 6 + d]
+        for face, corner in ((low, clow), (high, chigh)):
+            for slot in range(8):
+                face[slot, row:row + 8, :] = corner[n + slot]
         put_halo_rims(pl.ds(row, 8), clow[16 + y], chigh[16 + y], (xbh, xsrh, xsbh))
 
-    mains = {"black": (bm, xbm), "red": (rm, xrm), "sr": (srm, xsrm), "sb": (sbm, xsbm)}
+    mains = {"black": bm, "red": rm, "sr": srm, "sb": sbm}
     edges = {"black": (bh, xbh), "red": (rh, xrh), "sr": (srh, xsrh), "sb": (sbh, xsbh)}
 
     def main(kind, q):
-        own, halo = mains[kind]
         if 0 <= q < Q:
-            return own.at[q]
-        return halo.at[-1 - q if q < 0 else (2 if kind == "sb" else 3) + q - Q]
+            return mains[kind].at[q]
+        d = -1 - q if q < 0 else q - Q
+        if kind == "red":
+            return xrm.at[d if q < 0 else 3 + d]
+        return (low if q < 0 else high).at[SLOTS[kind] + d]
 
     def rim(kind, a):
         own, halo = edges[kind]
@@ -466,8 +482,8 @@
         (pltpu.with_memory_space_constraint(a.reshape(Q, 2, NY, NZ), pltpu.HBM), hbm()) for a in (field, source)
     ]
     edge = VM((4, ROWS, NZ), F32)
-    work, face, block = VM((Q, ROWS, NZ), F32), VM((Q, NY, NZ), F32), VM((Q, 2, NY, NZ), F32)
-    rows, strip, corner = VM((NY, NZ), F32), VM((26, 8, NZ), F32), VM((18, 8, NZ), F32)
+    work, block = VM((Q, ROWS, NZ), F32), VM((Q, 2, NY, NZ), F32)
+    rows, strip, corner = VM((NY, NZ), F32), VM((18, 8, NZ), F32), VM((18, 8, NZ), F32)
 
     fbuf, sbuf, zlow, zhigh = kernel(
         pack_kernel, 2, (block, block, rows, rows), [flip] + blocks,
@@ -475,7 +491,7 @@
     )
     zr = send(zlow, "gz", ring(nz, -1))
     zl = send(zhigh, "gz", ring(nz, 1))
-    bm, srm, sbm, high, low = kernel(face_kernel, 2, (work,) * 3 + (face,) * 2, [flip, fbuf, sbuf])
+    bm, srm, sbm, high, low = kernel(face_kernel, 2, (work,) * 5, [flip, fbuf, sbuf])
     high = send(high, "gx", chip)
     low = send(low, "gx", across)
     ylow, yhigh = kernel(y_kernel, 2, (strip, strip), [bm, srm, sbm, zr, zl])
@@ -499,15 +515,15 @@
         inner_kernel, 4, (work, work, edge, edge), [flip, bm, rm, srm, sbm, bh, rh, srh, sbh],
         input_output_aliases={1: 0, 2: 1, 5: 2, 6: 3},
     )
-    halo = [VM((n, ROWS, NZ), F32) for n in (6, 6, 4, 3, 3, 2)]
-    halos = kernel(halo_kernel, 2, halo, [(turn_of_halo, hbm()), high, low, ehigh, elow])
+    red, *halo = [VM((n, ROWS, NZ), F32) for n in (6, 3, 3, 2)]
+    halos = kernel(halo_kernel, 2, halo, [(turn_of_halo, hbm()), ehigh, elow])
     out = kernel(
         outer_kernel, 12,
-        [jax.ShapeDtypeStruct((Q, 2, NY, NZ), F32), work, work, edge, edge] + halo,
-        [flip, bm, rm, srm, sbm, bh, rh, srh, sbh, chigh, clow, *halos],
-        out_specs=[hbm()] + [pl.BlockSpec(memory_space=VM)] * 10,
-        input_output_aliases={1: 1, 2: 2, 5: 3, 6: 4, **{11 + i: 5 + i for i in range(6)}},
-        scratch_shapes=[halo[0], halo[3], block, pltpu.SemaphoreType.DMA((OUT_CHUNKS,))],
+        [jax.ShapeDtypeStruct((Q, 2, NY, NZ), F32), work, work, edge, edge, work, work] + halo,
+        [flip, bm, rm, srm, sbm, bh, rh, srh, sbh, chigh, clow, low, high, *halos],
+        out_specs=[hbm()] + [pl.BlockSpec(memory_space=VM)] * 9,
+        input_output_aliases={1: 1, 2: 2, 5: 3, 6: 4, **{11 + i: 5 + i for i in range(5)}},
+        scratch_shapes=[red, halo[0], block, pltpu.SemaphoreType.DMA((OUT_CHUNKS,))],
     )[0]
     return out.reshape(field.shape)
 

time: 56.8 us -> 57.9 us (1.019)
  waiting for transfers between devices: 19.4 us -> 21.7 us
  starting transfers between devices: 21.1 us -> 20.4 us
    ppermute x10, waiting for transfers between devices: 19.4 us -> 21.7 us  [send(): return lax.ppermute(near(value), axis, pairs)]
    ppermute x10, starting transfers between devices: 21.1 us -> 20.4 us  [send(): return lax.ppermute(near(value), axis, pairs)]
  transfers between devices with their start and end apart: 10 -> 10, of which waited for: 4 -> 4; matrix products, arithmetic and copies ran while one was open for 0% -> 0% of each run, Pallas kernels for 11% -> 10%
where the time goes in v4:
time: 57.9 us; the launch traced here: 57.7 us
  waiting for transfers between devices  21.7 us (37%)
  starting transfers between devices  20.4 us (35%)
  Pallas kernels  15.4 us (27%)
    ppermute x10, waiting for transfers between devices, send(): return lax.ppermute(near(value), axis, pairs)  21.7 us
    ppermute x10, starting transfers between devices, send(): return lax.ppermute(near(value), axis, pairs)  20.4 us
    pallas_call x9, Pallas kernels, kernel(): pl.pallas_call(body, out_shape=outs, in_specs=specs, out_specs=out_specs,...  15.4 us
  transfers between devices with their start and end apart: 10, of which 4 were waited for; matrix products, arithmetic and copies ran while one was open for 0% of the time, Pallas kernels for 10%

profile of v4, /device:TPU:1, one launch (start us, length us, event | category | flops | bytes accessed | tf_op | source)
XLA Modules:
  0.0 57.7 jit_solution(4483308563256073309)
XLA Ops:
  0.0 2.5 %shard_map.28 = (f32[8,2,256,128]{3,2,1,0:T(8,128)S(1)}, f32[8,2,256,128]{3,2,1,0:T(8,128)S(1)}, f32[256,128]{1,0:T(8,128)S(1)}, f32[256,128]{1,0:T(8,128)S(1)}) custom-call(s32[1]{0:T(128)} %bitcast.flip_ref, f32[8,2,256,128]{3,2,1,0:T(8,128)} %bitcast.4, f32[8,2,256,128]{3,2,1,0:T(8,128)} %bitcast.5), custom_call_target="tpu_custom_call" | custom-call | tf_op jit(solution)/shard_map/pallas_call | solution.py:462
  2.6 1.0 %shard_map.29 = (f32[8,288,128]{2,1,0:T(8,128)S(1)}, f32[8,288,128]{2,1,0:T(8,128)S(1)}, f32[8,288,128]{2,1,0:T(8,128)S(1)}, f32[8,288,128]{2,1,0:T(8,128)S(1)}, f32[8,288,128]{2,1,0:T(8,128)S(1)}) custom-call(s32[1]{0:T(128)} %bitcast.flip_ref, f32[8,2,256,128]{3,2,1,0:T(8,128)S(1)} %get-tuple-element.40.fbuf, f32[8,2,256,128]{3,2,1,0:T(8,128)S(1)} %get-tuple-element.41.sbuf), custom_call_target="tpu_custom_call" | custom-call | tf_op jit(solution)/shard_map/pallas_call | solution.py:462
  3.6 6.0 %collective-permute-start.6 = (f32[8,288,128]{2,1,0:T(8,128)S(1)}, f32[8,288,128]{2,1,0:T(8,128)S(1)}, u32[]{:S(2)}, u32[]{:S(2)}) collective-permute-start(f32[8,288,128]{2,1,0:T(8,128)S(1)} %get-tuple-element.67), channel_id=1, source_target_pairs={{32,64},{64,32},{33,65},{65,33},{34,66},{66,34},{35,67},{67,35},{3... | collective-permute-start | bytes 3538952 | tf_op jit(solution)/shard_map/ppermute | solution.py:468
  9.7 0.1 collective-permute-start.7
  9.7 3.9 %collective-permute-start = (f32[256,128]{1,0:T(8,128)S(1)}, f32[256,128]{1,0:T(8,128)S(1)}, u32[]{:S(2)}, u32[]{:S(2)}) collective-permute-start(f32[256,128]{1,0:T(8,128)S(1)} %get-tuple-element.45), channel_id=1, source_target_pairs={{0,7},{1,0},{2,1},{3,2},{4,3},{5,4},{6,5},{7,6},{8,15},{9,8},{10,9... | collective-permute-start | bytes 393224 | tf_op jit(solution)/shard_map/ppermute | solution.py:468
  13.6 0.0 collective-permute-start.1
  13.6 14.4 %collective-permute-done.zr = f32[256,128]{1,0:T(8,128)S(1)} collective-permute-done((f32[256,128]{1,0:T(8,128)S(1)}, f32[256,128]{1,0:T(8,128)S(1)}, u32[]{:S(2)}, u32[]{:S(2)}) %collective-permute-start) | collective-permute-done | bytes 131104 | tf_op jit(solution)/shard_map/ppermute | solution.py:468
  28.0 4.6 %collective-permute-done.1.zl = f32[256,128]{1,0:T(8,128)S(1)} collective-permute-done((f32[256,128]{1,0:T(8,128)S(1)}, f32[256,128]{1,0:T(8,128)S(1)}, u32[]{:S(2)}, u32[]{:S(2)}) %collective-permute-start.1) | collective-permute-done | bytes 131104 | tf_op jit(solution)/shard_map/ppermute | solution.py:468
  32.6 1.4 %collective-permute-start.3 = (f32[18,8,128]{2,1,0:T(8,128)S(1)}, f32[18,8,128]{2,1,0:T(8,128)S(1)}, u32[]{:S(2)}, u32[]{:S(2)}) collective-permute-start(f32[18,8,128]{2,1,0:T(8,128)S(1)} %get-tuple-element.48), channel_id=1, source_target_pairs={{0,8},{8,16},{16,24},{24,0},{1,9},{9,17},{17,25},{25,1},{2,10},{10... | collective-permute-start | bytes 221192 | tf_op jit(solution)/shard_map/ppermute | solution.py:468
  34.0 0.2 shard_map.34
  34.2 0.1 collective-permute-start.8
  34.3 1.5 %collective-permute-start.2 = (f32[18,8,128]{2,1,0:T(8,128)S(1)}, f32[18,8,128]{2,1,0:T(8,128)S(1)}, u32[]{:S(2)}, u32[]{:S(2)}) collective-permute-start(f32[18,8,128]{2,1,0:T(8,128)S(1)} %get-tuple-element.47.after), channel_id=1, source_target_pairs={{0,24},{8,0},{16,8},{24,16},{1,25},{9,1},{17,9},{25,17},{2,26},{10... | collective-permute-start | bytes 221192 | tf_op jit(solution)/shard_map/ppermute | solution.py:468
  35.8 1.4 %collective-permute-done.3.yl = f32[18,8,128]{2,1,0:T(8,128)S(1)} collective-permute-done((f32[18,8,128]{2,1,0:T(8,128)S(1)}, f32[18,8,128]{2,1,0:T(8,128)S(1)}, u32[]{:S(2)}, u32[]{:S(2)}) %collective-permute-start.3) | collective-permute-done | bytes 73760 | tf_op jit(solution)/shard_map/ppermute | solution.py:468
  37.2 5.2 %collective-permute-start.9 = (f32[256,128]{1,0:T(8,128)S(1)}, f32[256,128]{1,0:T(8,128)S(1)}, u32[]{:S(2)}, u32[]{:S(2)}) collective-permute-start(f32[256,128]{1,0:T(8,128)S(1)} %get-tuple-element.70), channel_id=1, source_target_pairs={{32,64},{64,32},{33,65},{65,33},{34,66},{66,34},{35,67},{67,35},{3... | collective-permute-start | bytes 393224 | tf_op jit(solution)/shard_map/ppermute | solution.py:468
  42.4 1.6 %shard_map.31 = (f32[8,288,128]{2,1,0:T(8,128)S(1)}, f32[8,288,128]{2,1,0:T(8,128)S(1)}, f32[4,288,128]{2,1,0:T(8,128)S(1)}, f32[4,288,128]{2,1,0:T(8,128)S(1)},...) custom-call(s32[1]{0:T(128)} %bitcast.flip_ref, ...), custom_call_target="tpu_custom_call", output_to_operand_aliasing={{0}: (4, {})} | custom-call | tf_op jit(solution)/shard_map/pallas_call | solution.py:462
  44.0 0.0 collective-permute-done.2.yr
  44.0 0.1 shard_map.32
  44.2 0.1 collective-permute-start.4
  44.2 0.0 collective-permute-done.8.ehigh
  44.3 2.1 %collective-permute-start.5 = (f32[18,8,128]{2,1,0:T(8,128)S(1)}, f32[18,8,128]{2,1,0:T(8,128)S(1)}, u32[]{:S(2)}, u32[]{:S(2)}) collective-permute-start(f32[18,8,128]{2,1,0:T(8,128)S(1)} %get-tuple-element.66.after), channel_id=1, source_target_pairs={{32,64},{64,32},{33,65},{65,33},{34,66},{66,34},{35,67},{67,35},{3... | collective-permute-start | bytes 221192 | tf_op jit(solution)/shard_map/ppermute | solution.py:468
  46.4 3.1 %shard_map.33 = (f32[8,288,128]{2,1,0:T(8,128)S(1)}, f32[8,288,128]{2,1,0:T(8,128)S(1)}, f32[4,288,128]{2,1,0:T(8,128)S(1)}, f32[4,288,128]{2,1,0:T(8,128)S(1)}) custom-call(s32[1]{0:T(128)} %bitcast.flip_ref, f32[8,288,128]{2,1,0:T(8,128)S(1)} %get-tuple-element.53.bm_in, ...), custom_call_target="tpu_custom_call", output_to_operand_aliasing={{0}: (1, {}), {1}: (2, {}), {2}: (5, {}), {3}: (6, {})} | custom-call | tf_op jit(solution)/shard_map/pallas_call | solution.py:462
  49.5 0.0 collective-permute-done.9.elow
  49.5 0.7 %shard_map.35 = (f32[3,288,128]{2,1,0:T(8,128)S(1)}, f32[3,288,128]{2,1,0:T(8,128)S(1)}, f32[2,288,128]{2,1,0:T(8,128)S(1)}) custom-call(f32[18,8,128]{2,1,0:T(8,128)S(1)} %get-tuple-element.66.after, f32[256,128]{1,0:T(8,128)S(1)} %collective-permute-done.8.ehigh, f32[256,128]{1,0:T(8,128)S(1)} %collective-permute-done.9.elow), custom_call_target="tpu_custom_call" | custom-call | tf_op jit(solution)/shard_map/pallas_call | solution.py:462
  50.2 0.0 collective-permute-done.4.chigh
  50.2 1.3 %collective-permute-done.5.clow = f32[18,8,128]{2,1,0:T(8,128)S(1)} collective-permute-done((f32[18,8,128]{2,1,0:T(8,128)S(1)}, f32[18,8,128]{2,1,0:T(8,128)S(1)}, u32[]{:S(2)}, u32[]{:S(2)}) %collective-permute-start.5) | collective-permute-done | bytes 73760 | tf_op jit(solution)/shard_map/ppermute | solution.py:468
  51.4 0.0 collective-permute-done.6.low_in
  51.4 0.0 collective-permute-done.7.high_in
  51.4 6.1 %shard_map.36 = (f32[8,2,256,128]{3,2,1,0:T(8,128)}, f32[8,288,128]{2,1,0:T(8,128)S(1)}, f32[8,288,128]{2,1,0:T(8,128)S(1)}, f32[4,288,128]{2,1,0:T(8,128)S(1)},...) custom-call(s32[1]{0:T(128)} %bitcast.flip_ref, ...), custom_call_target="tpu_custom_call", output_to_operand_aliasing={{1}: (1, {}), {2}: (2, {}), {3}: (5, {}), {4}: (6, {}), {5}... | custom-call | tf_op jit(solution)/shard_map/pallas_call | solution.py:462
  (1 shorter events, 0.0 us)
Async XLA Ops:
  3.6 47.8 %collective-permute-start.6 = (f32[8,288,128]{2,1,0:T(8,128)S(1)}, f32[8,288,128]{2,1,0:T(8,128)S(1)}, u32[]{:S(2)}, u32[]{:S(2)}) collective-permute-start(f32[8,288,128]{2,1,0:T(8,128)S(1)} %get-tuple-element.67), channel_id=1, source_target_pairs={{32,64},{64,32},{33,65},{65,33},{34,66},{66,34},{35,67},{67,35},{3... | collective-permute-start | bytes 3538952 | tf_op jit(solution)/shard_map/ppermute | solution.py:468
  9.7 41.8 %collective-permute-start.7 = (f32[8,288,128]{2,1,0:T(8,128)S(1)}, f32[8,288,128]{2,1,0:T(8,128)S(1)}, u32[]{:S(2)}, u32[]{:S(2)}) collective-permute-start(f32[8,288,128]{2,1,0:T(8,128)S(1)} %get-tuple-element.68), channel_id=1, source_target_pairs={{0,32},{32,0},{64,96},{96,64},{1,33},{33,1},{65,97},{97,65},{2,34}... | collective-permute-start | bytes 3538952 | tf_op jit(solution)/shard_map/ppermute | solution.py:468
  9.7 18.3 %collective-permute-start = (f32[256,128]{1,0:T(8,128)S(1)}, f32[256,128]{1,0:T(8,128)S(1)}, u32[]{:S(2)}, u32[]{:S(2)}) collective-permute-start(f32[256,128]{1,0:T(8,128)S(1)} %get-tuple-element.45), channel_id=1, source_target_pairs={{0,7},{1,0},{2,1},{3,2},{4,3},{5,4},{6,5},{7,6},{8,15},{9,8},{10,9... | collective-permute-start | bytes 393224 | tf_op jit(solution)/shard_map/ppermute | solution.py:468
  13.6 19.0 %collective-permute-start.1 = (f32[256,128]{1,0:T(8,128)S(1)}, f32[256,128]{1,0:T(8,128)S(1)}, u32[]{:S(2)}, u32[]{:S(2)}) collective-permute-start(f32[256,128]{1,0:T(8,128)S(1)} %get-tuple-element.46), channel_id=1, source_target_pairs={{0,1},{1,2},{2,3},{3,4},{4,5},{5,6},{6,7},{7,0},{8,9},{9,10},{10,1... | collective-permute-start | bytes 393224 | tf_op jit(solution)/shard_map/ppermute | solution.py:468
  32.6 4.5 %collective-permute-start.3 = (f32[18,8,128]{2,1,0:T(8,128)S(1)}, f32[18,8,128]{2,1,0:T(8,128)S(1)}, u32[]{:S(2)}, u32[]{:S(2)}) collective-permute-start(f32[18,8,128]{2,1,0:T(8,128)S(1)} %get-tuple-element.48), channel_id=1, source_target_pairs={{0,8},{8,16},{16,24},{24,0},{1,9},{9,17},{17,25},{25,1},{2,10},{10... | collective-permute-start | bytes 221192 | tf_op jit(solution)/shard_map/ppermute | solution.py:468
  34.2 10.0 %collective-permute-start.8 = (f32[256,128]{1,0:T(8,128)S(1)}, f32[256,128]{1,0:T(8,128)S(1)}, u32[]{:S(2)}, u32[]{:S(2)}) collective-permute-start(f32[256,128]{1,0:T(8,128)S(1)} %get-tuple-element.69), channel_id=1, source_target_pairs={{0,32},{32,0},{64,96},{96,64},{1,33},{33,1},{65,97},{97,65},{2,34}... | collective-permute-start | bytes 393224 | tf_op jit(solution)/shard_map/ppermute | solution.py:468
  34.3 9.7 %collective-permute-start.2 = (f32[18,8,128]{2,1,0:T(8,128)S(1)}, f32[18,8,128]{2,1,0:T(8,128)S(1)}, u32[]{:S(2)}, u32[]{:S(2)}) collective-permute-start(f32[18,8,128]{2,1,0:T(8,128)S(1)} %get-tuple-element.47.after), channel_id=1, source_target_pairs={{0,24},{8,0},{16,8},{24,16},{1,25},{9,1},{17,9},{25,17},{2,26},{10... | collective-permute-start | bytes 221192 | tf_op jit(solution)/shard_map/ppermute | solution.py:468
  37.2 12.3 %collective-permute-start.9 = (f32[256,128]{1,0:T(8,128)S(1)}, f32[256,128]{1,0:T(8,128)S(1)}, u32[]{:S(2)}, u32[]{:S(2)}) collective-permute-start(f32[256,128]{1,0:T(8,128)S(1)} %get-tuple-element.70), channel_id=1, source_target_pairs={{32,64},{64,32},{33,65},{65,33},{34,66},{66,34},{35,67},{67,35},{3... | collective-permute-start | bytes 393224 | tf_op jit(solution)/shard_map/ppermute | solution.py:468
  44.2 6.0 %collective-permute-start.4 = (f32[18,8,128]{2,1,0:T(8,128)S(1)}, f32[18,8,128]{2,1,0:T(8,128)S(1)}, u32[]{:S(2)}, u32[]{:S(2)}) collective-permute-start(f32[18,8,128]{2,1,0:T(8,128)S(1)} %get-tuple-element.65), channel_id=1, source_target_pairs={{0,32},{32,0},{64,96},{96,64},{1,33},{33,1},{65,97},{97,65},{2,34}... | collective-permute-start | bytes 221192 | tf_op jit(solution)/shard_map/ppermute | solution.py:468
  44.3 7.2 %collective-permute-start.5 = (f32[18,8,128]{2,1,0:T(8,128)S(1)}, f32[18,8,128]{2,1,0:T(8,128)S(1)}, u32[]{:S(2)}, u32[]{:S(2)}) collective-permute-start(f32[18,8,128]{2,1,0:T(8,128)S(1)} %get-tuple-element.66.after), channel_id=1, source_target_pairs={{32,64},{64,32},{33,65},{65,33},{34,66},{66,34},{35,67},{67,35},{3... | collective-permute-start | bytes 221192 | tf_op jit(solution)/shard_map/ppermute | solution.py:468
